TPU v7x, 32 devices: a whole 2x2x4 slice. The times are simulated.
32 devices in a mesh: replica: 8 (over z, core), tp: 4 (over y, x).
Axes of the slice: x: 2, y: 2, z: 4, core: 2. Of those that a mesh axis runs over, the one named last changes fastest.
Arguments:
- token_ids: int32 [128], replicated, may hold values from 0 to 8191
- embed_table: bfloat16 [8192, 8192], P('replica', 'tp'), may hold values from -6 to 6
- norm_gain: bfloat16 [8192], replicated, may hold values from 0.099609375 to 1.8984375
- w_query: bfloat16 [8192, 4096], P(('replica', 'tp')), may hold values from -0.0625 to 0.0625
- w_keyvalue: bfloat16 [8192, 2, 512], P(('replica', 'tp')), may hold values from -0.0625 to 0.0625
- key_cache: bfloat16 [512, 1024, 128], P(('replica', 'tp')), may hold values from -360 to 360
- value_cache: bfloat16 [512, 1024, 128], P(('replica', 'tp')), may hold values from -6 to 6
- cache_lengths: int32 [128], P('replica'), may hold values from 1 to 1024, as said below
Outputs:
- context: bfloat16 [512, 1024], P(('replica', 'tp'))
- query_weight_tp: bfloat16 [8192, 4096], P(None, 'tp')
- keyvalue_weight_tp: bfloat16 [8192, 2, 512], P(None, None, 'tp')
Inputs may be any that keep to these rules, and one draw needn't show every extreme that they name: `cache_lengths`: some sequence has exactly 1024 filled slots.
All inputs are finite; a program needn't handle non-finite values.
Results may differ from a plain program's by a relative error of at most 0.019.
The roundings to bfloat16 on the way count: a program that leaves them out, or rounds other values in their place, can miss the bound.
Values may be sent and summed in bfloat16 or wider, within the bound.
A program may use at most 128 MiB of HBM per device.

v0:
```python
import functools

import jax
import jax.numpy as jnp
from jax import lax
from jax.experimental import pallas as pl
from jax.experimental.pallas import tpu as pltpu
from jax.sharding import PartitionSpec as P


def attend(query, keys, values, key_new, value_new, lengths):
    scale = query.shape[-1] ** (-0.5)
    scores = jnp.einsum("rgd,rcd->rgc", query, keys, preferred_element_type=jnp.float32) * scale
    position = lax.broadcasted_iota(jnp.int32, scores.shape, 2)
    scores = jnp.where(position < lengths[:, None, None], scores, -jnp.inf)
    own = jnp.einsum("rgd,rd->rg", query, key_new, preferred_element_type=jnp.float32) * scale
    top = jnp.maximum(jnp.max(scores, axis=2), own)
    weights = jnp.exp(scores - top[:, :, None])
    own_weight = jnp.exp(own - top)
    total = jnp.sum(weights, axis=2) + own_weight
    weights = (weights / total[:, :, None]).astype(jnp.bfloat16)
    own_weight = (own_weight / total).astype(jnp.bfloat16)
    context = jnp.einsum("rgc,rcd->rgd", weights, values, preferred_element_type=jnp.float32)
    context = (
        context
        + own_weight.astype(jnp.float32)[:, :, None] * value_new.astype(jnp.float32)[:, None, :]
    )
    return context.astype(jnp.bfloat16)


def per_device(
    token_ids, embed_table, norm_gain, w_query, w_keyvalue, key_cache, value_cache, cache_lengths
):
    group_index = lax.axis_index("replica")
    tp_index = lax.axis_index("tp")
    vocab_rows, feature_cols = embed_table.shape
    batch = cache_lengths.shape[0]
    first_id = group_index * vocab_rows
    picked = token_ids - first_id
    columns = lax.broadcasted_iota(jnp.int32, (batch * lax.axis_size("replica"), vocab_rows), 1)
    onehot = (picked[:, None] == columns).astype(jnp.bfloat16)
    embedded = lax.psum_scatter(
        jnp.dot(onehot, embed_table, preferred_element_type=jnp.float32),
        "replica",
        scatter_dimension=0,
        tiled=True,
    ).astype(jnp.bfloat16)
    whole = lax.all_gather(embedded, "tp", axis=1, tiled=True)
    values32 = whole.astype(jnp.float32)
    mean_square = jnp.mean(values32 * values32, axis=1, keepdims=True)
    normed = (values32 * lax.rsqrt(mean_square + 1e-05) * norm_gain.astype(jnp.float32)).astype(
        jnp.bfloat16
    )
    width = normed.shape[1]
    query_rows = w_query.reshape(w_query.shape[0], 1, w_query.shape[1])
    query_mid, pair_mid = (
        lax.all_to_all(query_rows, "tp", split_axis=2, concat_axis=0, tiled=True),
        lax.all_to_all(w_keyvalue, "tp", split_axis=2, concat_axis=0, tiled=True),
    )
    flat_query = query_mid.reshape(query_mid.shape[0], query_mid.shape[2])
    pair_cols = pair_mid.shape[2]
    flat_pair = pair_mid.reshape(pair_mid.shape[0], 2 * pair_cols)
    query_full, pair_full = (
        lax.all_gather(flat_query, "replica", axis=0, tiled=True),
        lax.all_gather(flat_pair, "replica", axis=0, tiled=True),
    )
    query_acc = jnp.dot(normed, query_full, preferred_element_type=jnp.float32)
    pair_acc = jnp.dot(normed, pair_full, preferred_element_type=jnp.float32)
    query_local = query_acc.astype(jnp.bfloat16)
    pair_local = pair_acc.astype(jnp.bfloat16).reshape(batch, 2, pair_cols)
    query_heads, pair_heads = (
        lax.all_gather(query_local, "tp", axis=1, tiled=True),
        lax.all_gather(pair_local, "tp", axis=2, tiled=True),
    )
    head_size = key_cache.shape[2]
    kv_heads = pair_heads.shape[2] // head_size
    group = query_heads.shape[1] // (kv_heads * head_size)
    rows_here = key_cache.shape[0]
    first_row = tp_index * rows_here
    query_grouped = (
        query_heads.reshape(batch, kv_heads, group, head_size)
        .transpose(1, 0, 2, 3)
        .reshape(kv_heads * batch, group, head_size)
    )
    key_grouped = (
        pair_heads[:, 0]
        .reshape(batch, kv_heads, head_size)
        .transpose(1, 0, 2)
        .reshape(kv_heads * batch, head_size)
    )
    value_grouped = (
        pair_heads[:, 1]
        .reshape(batch, kv_heads, head_size)
        .transpose(1, 0, 2)
        .reshape(kv_heads * batch, head_size)
    )
    query_mine = lax.dynamic_slice_in_dim(query_grouped, first_row, rows_here, 0)
    key_mine = lax.dynamic_slice_in_dim(key_grouped, first_row, rows_here, 0)
    value_mine = lax.dynamic_slice_in_dim(value_grouped, first_row, rows_here, 0)
    sequence = (first_row + lax.broadcasted_iota(jnp.int32, (rows_here,), 0)) % batch
    matches = sequence[:, None] == lax.broadcasted_iota(jnp.int32, (rows_here, batch), 1)
    row_lengths = jnp.sum(jnp.where(matches, cache_lengths[None, :], 0), axis=1)
    context = attend(query_mine, key_cache, value_cache, key_mine, value_mine, row_lengths)
    context = context.reshape(rows_here, group * head_size)
    return (context, query_full, pair_full.reshape(width, 2, pair_cols))


MESH = pl.DeviceIdType.MESH


def exchange_kernel(
    planes,
    token_ref,
    gain_ref,
    table_ref,
    query_ref,
    pair_ref,
    query_out,
    pair_out,
    normed_ref,
    spread_ref,
    query_hold,
    pair_hold,
    table_hold,
    part_ref,
    given,
    joined,
    picked,
    pieces,
    send_sem,
    recv_sem,
    plane_sem,
    local_sem,
    give_send,
    give_recv,
    pick_send,
    pick_recv,
    piece_send,
    piece_recv,
):
    r, t = lax.axis_index("replica"), lax.axis_index("tp")
    replicas = 2 * planes
    z, k = r // 2, lax.rem(r, 2)
    ty, tx = t // 2, lax.rem(t, 2)
    rows, query_cols = query_hold.shape
    pair_cols = pair_hold.shape[2]
    batch, feats = picked.shape[1], picked.shape[2]
    other = [t, ty * 2 + 1 - tx, (1 - ty) * 2 + tx, 3 - t]
    partner = z * 2 + 1 - k
    width = replicas * 4 * rows

    barrier = pltpu.get_barrier_semaphore()
    for step in range(1, replicas):
        pl.semaphore_signal(
            barrier, inc=1, device_id=(lax.rem(r + step, replicas), t), device_id_type=MESH
        )
    for j in range(1, 4):
        pl.semaphore_signal(barrier, inc=1, device_id=(r, other[j]), device_id_type=MESH)
    pl.semaphore_wait(barrier, replicas - 1 + 3)

    def piece_id(plane, core, tp):
        return (plane * 2 + core) * 4 + tp

    def rows_of(ref, pid):
        where = pl.ds(pl.multiple_of(pid * rows, rows), rows)
        return ref.at[where]

    def columns(tp):
        return (
            query_ref.at[:, pl.ds(pl.multiple_of(tp * query_cols, query_cols), query_cols)],
            pair_ref.at[:, :, pl.ds(pl.multiple_of(tp * pair_cols, pair_cols), pair_cols)],
        )

    def copies(pid, sources, way, slot, target):
        made = []
        for c, (source, out) in enumerate(zip(sources, (query_out, pair_out))):
            sem = plane_sem.at[c, slot] if way is None else send_sem.at[c, way, slot]
            made.append(
                pltpu.make_async_remote_copy(
                    src_ref=source,
                    dst_ref=rows_of(out, pid),
                    send_sem=sem,
                    recv_sem=recv_sem.at[c, pid],
                    device_id=target,
                    device_id_type=MESH,
                )
            )
        return made

    def landed(pid):
        for c, out in enumerate((query_out, pair_out)):
            pltpu.make_async_copy(
                rows_of(out, pid), rows_of(out, pid), recv_sem.at[c, pid]
            ).wait()

    def onward(pid, sources, slot, up, down, wait=False):
        def act(made):
            for copy in made:
                copy.wait_send() if wait else copy.start()

        if up:

            @pl.when(z < planes - 1)
            def _():
                act(copies(pid, sources, 0, slot, (lax.rem(r + 2, replicas), t)))

        if down:

            @pl.when(z > 0)
            def _():
                act(copies(pid, sources, 1, slot, (lax.rem(r + replicas - 2, replicas), t)))

        act(copies(pid, sources, 2, slot, (partner, t)))

    def stored(pid):
        return rows_of(query_out, pid), rows_of(pair_out, pid)

    mine = piece_id(z, k, t)
    sources = columns(t)
    bring = [
        pltpu.make_async_copy(sources[0], query_hold, local_sem.at[0]),
        pltpu.make_async_copy(sources[1], pair_hold, local_sem.at[1]),
    ]
    across = [copies(mine, columns(other[j]), None, j - 1, (r, other[j])) for j in range(1, 4)]
    for made in across:
        for copy in made:
            copy.start()
    onward(mine, sources, 0, True, True)
    for copy in bring:
        copy.start()

    table = pltpu.make_async_copy(table_ref, table_hold, local_sem.at[2])
    table.start()
    gives = [
        pltpu.make_async_remote_copy(
            src_ref=part_ref.at[plane, 1 - k],
            dst_ref=given.at[plane],
            send_sem=give_send.at[plane],
            recv_sem=give_recv.at[plane],
            device_id=(partner, t),
            device_id_type=MESH,
        )
        for plane in range(planes)
    ]
    picks = []
    for far in range(1, planes):
        plane = lax.rem(z + far, planes)
        picks.append(
            pltpu.make_async_remote_copy(
                src_ref=joined.at[plane],
                dst_ref=picked.at[far - 1],
                send_sem=pick_send.at[far - 1],
                recv_sem=pick_recv.at[far - 1],
                device_id=(plane * 2 + k, t),
                device_id_type=MESH,
            )
        )
    for copy in bring:
        copy.wait()
    put = [
        pltpu.make_async_copy(query_hold, rows_of(query_out, mine), local_sem.at[3]),
        pltpu.make_async_copy(pair_hold, rows_of(pair_out, mine), local_sem.at[4]),
    ]
    for copy in put:
        copy.start()

    gather = [
        pltpu.make_async_remote_copy(
            src_ref=pieces.at[t],
            dst_ref=pieces.at[t],
            send_sem=piece_send.at[j - 1],
            recv_sem=piece_recv.at[j - 1],
            device_id=(r, other[j]),
            device_id_type=MESH,
        )
        for j in range(1, 4)
    ]

    def select_rows():
        table.wait()
        vocab_rows = table_hold.shape[0]
        tokens = token_ref.shape[0]
        columns = lax.broadcasted_iota(jnp.int32, (tokens, vocab_rows), 1)
        onehot = (token_ref[...] - r * vocab_rows == columns).astype(jnp.bfloat16)
        block = 256

        def select(i, carry):
            where = pl.ds(pl.multiple_of(i * block, block), block)
            rows_here = jnp.dot(
                onehot, table_hold[:, where], preferred_element_type=jnp.float32
            ).astype(jnp.bfloat16)
            part_ref[:, :, :, where] = rows_here.reshape(planes, 2, batch, block)
            return carry

        lax.fori_loop(0, feats // block, select, 0)

    def join():
        for copy in gives:
            copy.wait()
        for plane in range(planes):
            own = part_ref[plane, k].astype(jnp.float32)
            joined[plane] = (own + given[plane].astype(jnp.float32)).astype(jnp.bfloat16)

    def sum_picks():
        for copy in picks:
            copy.wait()
        total = joined[z].astype(jnp.float32)
        for far in range(1, planes):
            total = total + picked[far - 1].astype(jnp.float32)
        pieces[t] = total.astype(jnp.bfloat16)

    def normalise():
        for copy in gather:
            copy.wait()
        square = jnp.zeros((batch, 1), jnp.float32)
        for i in range(4):
            part = pieces[i].astype(jnp.float32)
            square = square + jnp.sum(part * part, axis=1, keepdims=True)
        factor = lax.rsqrt(square / (4 * feats) + 1e-05)
        for i in range(4):
            part = pieces[i].astype(jnp.float32)
            gain = gain_ref[:, i * feats : (i + 1) * feats].astype(jnp.float32)
            normed_ref[:, i * feats : (i + 1) * feats] = (part * factor * gain).astype(
                jnp.bfloat16
            )
        block = 256
        line = lax.broadcasted_iota(jnp.int32, (block, 2 * block), 0)
        column = lax.broadcasted_iota(jnp.int32, (block, 2 * block), 1)
        even = (column == 2 * line).astype(jnp.bfloat16)
        odd = (column == 2 * line + 1).astype(jnp.bfloat16)

        def spread(i, carry):
            part = normed_ref[:, pl.ds(pl.multiple_of(i * block, block), block)]
            where = pl.ds(pl.multiple_of(i * 2 * block, 2 * block), 2 * block)
            spread_ref[0:batch, where] = jnp.dot(
                part, even, preferred_element_type=jnp.float32
            ).astype(jnp.bfloat16)
            spread_ref[batch : 2 * batch, where] = jnp.dot(
                part, odd, preferred_element_type=jnp.float32
            ).astype(jnp.bfloat16)
            return carry

        lax.fori_loop(0, 4 * feats // block, spread, 0)

    steps = 4 * (planes - 1)
    for step in range(steps):
        if 0 < step < 4:
            pid = piece_id(z, k, other[step])
            landed(pid)
            onward(pid, stored(pid), step, True, True)
        far, j = step // 4 + 1, step % 4

        @pl.when(z >= far)
        def _():
            pid = piece_id(lax.rem(z + planes - far, planes), k, other[j])
            landed(pid)
            onward(pid, stored(pid), 4 * far + j, True, False)

        @pl.when(z + far < planes)
        def _():
            pid = piece_id(lax.rem(z + far, planes), k, other[j])
            landed(pid)
            onward(pid, stored(pid), 4 * (planes - 1 + far) + j, False, True)

        if step == 0:
            select_rows()
        if step == 1:
            for copy in gives:
                copy.start()
        if step == 2:
            join()
        if step == 3:
            for copy in picks:
                copy.start()
        if step == 7:
            sum_picks()
        if step == 8:
            for copy in gather:
                copy.start()
        if step == 9:
            normalise()

    for copy in put:
        copy.wait()
    for made in across:
        for copy in made:
            copy.wait_send()
    onward(mine, sources, 0, True, True, wait=True)
    for j in range(1, 4):
        pid = piece_id(z, k, other[j])
        onward(pid, stored(pid), j, True, True, wait=True)
    for step in range(steps):
        far, j = step // 4 + 1, step % 4

        @pl.when(z >= far)
        def _():
            pid = piece_id(lax.rem(z + planes - far, planes), k, other[j])
            onward(pid, stored(pid), 4 * far + j, True, False, wait=True)

        @pl.when(z + far < planes)
        def _():
            pid = piece_id(lax.rem(z + far, planes), k, other[j])
            onward(pid, stored(pid), 4 * (planes - 1 + far) + j, False, True, wait=True)

    for plane in range(planes):
        for j in range(4):
            landed(piece_id(plane, 1 - k, j))


def exchange(token_ids, norm_gain, embed_table, w_query, w_keyvalue, planes, batch):
    rows, all_query = w_query.shape
    query_cols, pair_cols = all_query // 4, w_keyvalue.shape[2] // 4
    replicas = 2 * planes
    width = rows * replicas * 4
    feats = embed_table.shape[1]
    kind = w_query.dtype
    anywhere = pl.BlockSpec(memory_space=pl.ANY)
    vmem = pl.BlockSpec(memory_space=pltpu.VMEM)
    hbm = pl.BlockSpec(memory_space=pltpu.HBM)
    dma = pltpu.SemaphoreType.DMA
    slots = 4 * (2 * planes - 1)
    return pl.pallas_call(
        functools.partial(exchange_kernel, planes),
        out_shape=(
            jax.ShapeDtypeStruct((width, query_cols), w_query.dtype),
            jax.ShapeDtypeStruct((width, 2, pair_cols), w_query.dtype),
            jax.ShapeDtypeStruct((batch, width), w_query.dtype),
            jax.ShapeDtypeStruct((2 * batch, 2 * width), w_query.dtype),
        ),
        in_specs=[vmem, vmem, hbm, hbm, hbm],
        out_specs=(anywhere, anywhere, vmem, vmem),
        scratch_shapes=[
            pltpu.VMEM((rows, query_cols), w_query.dtype),
            pltpu.VMEM((rows, 2, pair_cols), w_query.dtype),
            pltpu.VMEM(embed_table.shape, kind),
            pltpu.VMEM((planes, 2, batch, feats), kind),
            pltpu.VMEM((planes, batch, feats), kind),
            pltpu.VMEM((planes, batch, feats), kind),
            pltpu.VMEM((planes - 1, batch, feats), kind),
            pltpu.VMEM((4, batch, feats), kind),
            dma((2, 3, slots)),
            dma((2, replicas * 4)),
            dma((2, 3)),
            dma((5,)),
            dma((planes,)),
            dma((planes,)),
            dma((planes - 1,)),
            dma((planes - 1,)),
            dma((3,)),
            dma((3,)),
        ],
        compiler_params=pltpu.CompilerParams(
            collective_id=0, has_side_effects=True, vmem_limit_bytes=20 * 2**20
        ),
        cost_estimate=pl.CostEstimate(
            flops=2 * 10**11, bytes_accessed=2 * width * query_cols, transcendentals=0
        ),
        name="weight_exchange",
    )(token_ids.reshape(-1, 1), norm_gain.reshape(1, -1), embed_table, w_query, w_keyvalue)


def project_kernel(
    normed_ref,
    spread_ref,
    query_in,
    pair_in,
    query_all,
    pair_all,
    query_ref,
    pair_ref,
    q_ref,
    kv_ref,
    q_acc,
    kv_acc,
    sems,
):
    step = pl.program_id(0)
    stores = [
        pltpu.make_async_copy(query_all, query_ref, sems.at[0]),
        pltpu.make_async_copy(pair_all, pair_ref, sems.at[1]),
    ]

    @pl.when(step == 0)
    def _():
        for copy in stores:
            copy.start()
        q_acc[...] = jnp.zeros_like(q_acc)
        kv_acc[...] = jnp.zeros_like(kv_acc)

    q_acc[...] += jnp.dot(normed_ref[...], query_in[...], preferred_element_type=jnp.float32)
    kv_acc[...] += jnp.dot(spread_ref[...], pair_in[...], preferred_element_type=jnp.float32)

    @pl.when(step == pl.num_programs(0) - 1)
    def _():
        q_ref[...] = q_acc[...].astype(q_ref.dtype)
        kv_ref[...] = kv_acc[...].astype(kv_ref.dtype)
        for copy in stores:
            copy.wait()


def project(normed, spread, query_all, pair_all):
    batch, width = normed.shape
    query_cols, pair_cols = query_all.shape[1], pair_all.shape[2]
    pair_flat = pair_all.reshape(2 * width, pair_cols)
    block = 512
    anywhere = pl.BlockSpec(memory_space=pl.ANY)
    hbm = pl.BlockSpec(memory_space=pltpu.HBM)
    query_spec = pl.BlockSpec((block, query_cols), lambda i: (i, 0))
    pair_spec = pl.BlockSpec((2 * block, pair_cols), lambda i: (i, 0))
    query_out, pair_out, query, pair = pl.pallas_call(
        project_kernel,
        grid=(width // block,),
        out_shape=(
            jax.ShapeDtypeStruct(query_all.shape, query_all.dtype),
            jax.ShapeDtypeStruct(pair_flat.shape, pair_all.dtype),
            jax.ShapeDtypeStruct((batch, query_cols), normed.dtype),
            jax.ShapeDtypeStruct((2 * batch, pair_cols), normed.dtype),
        ),
        in_specs=[
            pl.BlockSpec((batch, block), lambda i: (0, i)),
            pl.BlockSpec((2 * batch, 2 * block), lambda i: (0, i)),
            query_spec,
            pair_spec,
            anywhere,
            anywhere,
        ],
        out_specs=(
            hbm,
            hbm,
            pl.BlockSpec((batch, query_cols), lambda i: (0, 0)),
            pl.BlockSpec((2 * batch, pair_cols), lambda i: (0, 0)),
        ),
        scratch_shapes=[
            pltpu.VMEM((batch, query_cols), jnp.float32),
            pltpu.VMEM((2 * batch, pair_cols), jnp.float32),
            pltpu.SemaphoreType.DMA((2,)),
        ],
        compiler_params=pltpu.CompilerParams(vmem_limit_bytes=16 * 2**20),
        cost_estimate=pl.CostEstimate(
            flops=2 * batch * width * (query_cols + 4 * pair_cols),
            bytes_accessed=4 * width * (query_cols + 2 * pair_cols),
            transcendentals=0,
        ),
        name="project_and_store",
    )(normed, spread, query_all, pair_flat, query_all, pair_flat)
    return query_out, pair_out.reshape(width, 2, pair_cols), query, pair


def per_device_line(
    planes,
    token_ids,
    embed_table,
    norm_gain,
    w_query,
    w_keyvalue,
    key_cache,
    value_cache,
    cache_lengths,
):
    batch = cache_lengths.shape[0]
    head_size = key_cache.shape[2]
    query_all, pair_all, normed, spread = exchange(
        token_ids, norm_gain, embed_table, w_query, w_keyvalue, planes, batch
    )
    query_out, pair_out, query, pair = project(normed, spread, query_all, pair_all)
    query = query.reshape(batch, -1, head_size)
    context = attend(query, key_cache, value_cache, pair[:batch], pair[batch:], cache_lengths)
    return context.reshape(batch, -1), query_out, pair_out


def solution(mesh):
    replicas, tp = mesh.shape["replica"], mesh.shape["tp"]

    def body(*args):
        key_cache, lengths, w_keyvalue = args[5], args[7], args[4]
        one_head = w_keyvalue.shape[2] == tp * key_cache.shape[2]
        own_rows = key_cache.shape[0] == lengths.shape[0]
        if tp == 4 and replicas % 2 == 0 and replicas > 6 and one_head and own_rows:
            return per_device_line(replicas // 2, *args)
        return per_device(*args)

    return jax.shard_map(
        body,
        mesh=mesh,
        in_specs=(
            P(),
            P("replica", "tp"),
            P(),
            P(("replica", "tp"), None),
            P(("replica", "tp"), None, None),
            P(("replica", "tp"), None, None),
            P(("replica", "tp"), None, None),
            P("replica"),
        ),
        out_specs=(P(("replica", "tp"), None), P(None, "tp"), P(None, None, "tp")),
        check_vma=False,
    )
```

profile of v0, /device:TPU:1, one launch (start us, length us, event | category | flops | bytes accessed | tf_op | source)
XLA Modules:
  0.0 204.0 jit_solution(8519001430999846309)
XLA Ops:
  0.6 0.7 reshape.30.gain_ref
  1.4 0.8 copy.11.token_ref
  2.1 0.0 copy-start
  2.1 2.2 %copy-done = bf16[1024,2048]{1,0:T(8,128)(2,1)S(1)} copy-done((bf16[1024,2048]{1,0:T(8,128)(2,1)S(1)}, bf16[1024,2048]{1,0:T(8,128)(2,1)}, u32[]{:S(2)}) %copy-start) | copy-done | bytes 4194328
  4.3 0.0 copy-start.1
  4.3 1.6 copy-done.1
  5.9 0.0 copy-start.2
  5.9 1.0 copy-done.2
  7.0 185.2 %weight_exchange.1 = (bf16[8192,1024]{1,0:T(8,128)(2,1)S(1)}, bf16[8192,2,128]{2,1,0:T(2,128)(2,1)S(1)}, bf16[16,8192]{1,0:T(8,128)(2,1)S(1)}, bf16[32,16384]{1,0:T(8,128)(2,1)S(1)}) custom-call(s32[128,1]{1,0:T(8,128)S(1)} %copy.11.token_ref, bf16[1,8192]{1,0:T(2,128)(2,1)S(1)} %reshape.30.gain_ref, bf16[1024,2048]{1,0:T(8,128)(2,1)S(1)} %copy-done, ...), custom_call_target="tpu_custom_call" | custom-call | flops 199999995904 | bytes 16777216 | tf_op jit(solution)/shard_map/weight_exchange/pallas_call | solution.py:422
  192.1 0.0 copy-start.3
  192.1 0.0 copy-start.5
  192.1 8.3 %project_and_store.1 = (bf16[8192,1024]{1,0:T(8,128)(2,1)}, bf16[16384,128]{1,0:T(8,128)(2,1)}, bf16[16,1024]{1,0:T(8,128)(2,1)S(1)}, bf16[32,128]{1,0:T(8,128)(2,1)S(1)}) custom-call(bf16[16,8192]{1,0:T(8,128)(2,1)S(1)} %get-tuple-element.11.normed_ref, bf16[32,16384]{1,0:T(8,128)(2,1)S(1)} %get-tuple-element.12.spread_ref, ...), custom_call_target="tpu_custom_call" | custom-call | flops 402653184 | bytes 41943040 | tf_op jit(solution)/shard_map/project_and_store/pallas_call | solution.py:510
  200.5 0.0 copy-start.4
  200.5 0.1 fusion.5
  200.6 0.0 copy-done.3
  200.6 0.0 copy-done.5
  200.7 1.3 fusion.9
  201.9 0.2 fusion.2
  202.2 0.5 copy-done.4
  202.7 0.7 fusion.1
  203.4 0.6 copy.19
  (4 shorter events, 0.0 us)
Async XLA Ops:
  2.1 2.2 %copy-start = (bf16[1024,2048]{1,0:T(8,128)(2,1)S(1)}, bf16[1024,2048]{1,0:T(8,128)(2,1)}, u32[]{:S(2)}) copy-start(bf16[1024,2048]{1,0:T(8,128)(2,1)} %table_ref.1) | copy-start | bytes 12582916
  4.3 1.6 copy-start.1
  5.9 1.0 copy-start.2
  192.1 8.5 %copy-start.3 = (bf16[16,1024,128]{2,1,0:T(8,128)(2,1)S(1)}, bf16[16,1024,128]{2,1,0:T(8,128)(2,1)}, u32[]{:S(2)}) copy-start(bf16[16,1024,128]{2,1,0:T(8,128)(2,1)} %param.13) | copy-start | bytes 12582916
  192.1 8.5 %copy-start.5 = (s32[16]{0:T(128)S(1)}, s32[16]{0:T(128)}, u32[]{:S(2)}) copy-start(s32[16]{0:T(128)} %param.15) | copy-start | bytes 196
  200.5 2.2 %copy-start.4 = (bf16[16,1024,128]{2,1,0:T(8,128)(2,1)S(1)}, bf16[16,1024,128]{2,1,0:T(8,128)(2,1)}, u32[]{:S(2)}) copy-start(bf16[16,1024,128]{2,1,0:T(8,128)(2,1)} %param.14) | copy-start | bytes 12582916
where the time goes:
time: 205 us; the launch traced here: 204 us
  Pallas kernels  193 us (94%)
  local copies, waits for them, and re-layouts  7.45 us (4%)
  matrix products  2.12 us (1%)
    pallas_call x1, Pallas kernels, exchange(): pl.pallas_call(functools.partial(exchange_kernel, planes), out_shape=(jax...  185 us
    pallas_call x1, Pallas kernels, project(): pl.pallas_call(project_kernel, grid=(width // block,), out_shape=(jax.Sha...  8.32 us
    unnamed x14, local copies, waits for them, and re-layouts  5.95 us

commit v1 on v0

v1 whole, which is shorter than its diff:
```python
import functools

import jax
import jax.numpy as jnp
from jax import lax
from jax.experimental import pallas as pl
from jax.experimental.pallas import tpu as pltpu
from jax.sharding import PartitionSpec as P


def attend(query, keys, values, key_new, value_new, lengths):
    scale = query.shape[-1] ** (-0.5)
    scores = jnp.einsum("rgd,rcd->rgc", query, keys, preferred_element_type=jnp.float32) * scale
    position = lax.broadcasted_iota(jnp.int32, scores.shape, 2)
    scores = jnp.where(position < lengths[:, None, None], scores, -jnp.inf)
    own = jnp.einsum("rgd,rd->rg", query, key_new, preferred_element_type=jnp.float32) * scale
    top = jnp.maximum(jnp.max(scores, axis=2), own)
    weights = jnp.exp(scores - top[:, :, None])
    own_weight = jnp.exp(own - top)
    total = jnp.sum(weights, axis=2) + own_weight
    weights = (weights / total[:, :, None]).astype(jnp.bfloat16)
    own_weight = (own_weight / total).astype(jnp.bfloat16)
    context = jnp.einsum("rgc,rcd->rgd", weights, values, preferred_element_type=jnp.float32)
    context = (
        context
        + own_weight.astype(jnp.float32)[:, :, None] * value_new.astype(jnp.float32)[:, None, :]
    )
    return context.astype(jnp.bfloat16)


def per_device(
    token_ids, embed_table, norm_gain, w_query, w_keyvalue, key_cache, value_cache, cache_lengths
):
    group_index = lax.axis_index("replica")
    tp_index = lax.axis_index("tp")
    vocab_rows, feature_cols = embed_table.shape
    batch = cache_lengths.shape[0]
    first_id = group_index * vocab_rows
    picked = token_ids - first_id
    columns = lax.broadcasted_iota(jnp.int32, (batch * lax.axis_size("replica"), vocab_rows), 1)
    onehot = (picked[:, None] == columns).astype(jnp.bfloat16)
    embedded = lax.psum_scatter(
        jnp.dot(onehot, embed_table, preferred_element_type=jnp.float32),
        "replica",
        scatter_dimension=0,
        tiled=True,
    ).astype(jnp.bfloat16)
    whole = lax.all_gather(embedded, "tp", axis=1, tiled=True)
    values32 = whole.astype(jnp.float32)
    mean_square = jnp.mean(values32 * values32, axis=1, keepdims=True)
    normed = (values32 * lax.rsqrt(mean_square + 1e-05) * norm_gain.astype(jnp.float32)).astype(
        jnp.bfloat16
    )
    width = normed.shape[1]
    query_rows = w_query.reshape(w_query.shape[0], 1, w_query.shape[1])
    query_mid, pair_mid = (
        lax.all_to_all(query_rows, "tp", split_axis=2, concat_axis=0, tiled=True),
        lax.all_to_all(w_keyvalue, "tp", split_axis=2, concat_axis=0, tiled=True),
    )
    flat_query = query_mid.reshape(query_mid.shape[0], query_mid.shape[2])
    pair_cols = pair_mid.shape[2]
    flat_pair = pair_mid.reshape(pair_mid.shape[0], 2 * pair_cols)
    query_full, pair_full = (
        lax.all_gather(flat_query, "replica", axis=0, tiled=True),
        lax.all_gather(flat_pair, "replica", axis=0, tiled=True),
    )
    query_acc = jnp.dot(normed, query_full, preferred_element_type=jnp.float32)
    pair_acc = jnp.dot(normed, pair_full, preferred_element_type=jnp.float32)
    query_local = query_acc.astype(jnp.bfloat16)
    pair_local = pair_acc.astype(jnp.bfloat16).reshape(batch, 2, pair_cols)
    query_heads, pair_heads = (
        lax.all_gather(query_local, "tp", axis=1, tiled=True),
        lax.all_gather(pair_local, "tp", axis=2, tiled=True),
    )
    head_size = key_cache.shape[2]
    kv_heads = pair_heads.shape[2] // head_size
    group = query_heads.shape[1] // (kv_heads * head_size)
    rows_here = key_cache.shape[0]
    first_row = tp_index * rows_here
    query_grouped = (
        query_heads.reshape(batch, kv_heads, group, head_size)
        .transpose(1, 0, 2, 3)
        .reshape(kv_heads * batch, group, head_size)
    )
    key_grouped = (
        pair_heads[:, 0]
        .reshape(batch, kv_heads, head_size)
        .transpose(1, 0, 2)
        .reshape(kv_heads * batch, head_size)
    )
    value_grouped = (
        pair_heads[:, 1]
        .reshape(batch, kv_heads, head_size)
        .transpose(1, 0, 2)
        .reshape(kv_heads * batch, head_size)
    )
    query_mine = lax.dynamic_slice_in_dim(query_grouped, first_row, rows_here, 0)
    key_mine = lax.dynamic_slice_in_dim(key_grouped, first_row, rows_here, 0)
    value_mine = lax.dynamic_slice_in_dim(value_grouped, first_row, rows_here, 0)
    sequence = (first_row + lax.broadcasted_iota(jnp.int32, (rows_here,), 0)) % batch
    matches = sequence[:, None] == lax.broadcasted_iota(jnp.int32, (rows_here, batch), 1)
    row_lengths = jnp.sum(jnp.where(matches, cache_lengths[None, :], 0), axis=1)
    context = attend(query_mine, key_cache, value_cache, key_mine, value_mine, row_lengths)
    context = context.reshape(rows_here, group * head_size)
    return (context, query_full, pair_full.reshape(width, 2, pair_cols))


MESH = pl.DeviceIdType.MESH


def exchange_kernel(
    planes,
    subs,
    token_in,
    gain_in,
    length_in,
    table_in,
    query_in,
    pair_in,
    key_in,
    value_in,
    query_out,
    pair_out,
    key_out,
    value_out,
    length_out,
    normed_ref,
    spread_ref,
    token_hold,
    gain_hold,
    gain_wide,
    length_hold,
    table_hold,
    onehot_ref,
    part_ref,
    given,
    joined,
    picked,
    relayed,
    relay_sum,
    relay_in,
    pieces,
    send_sem,
    recv_sem,
    across_sem,
    local_sem,
    give_send,
    give_recv,
    pick_send,
    pick_recv,
    relay_send,
    relay_recv,
    piece_send,
    piece_recv,
):
    r, t = lax.axis_index("replica"), lax.axis_index("tp")
    replicas = 2 * planes
    z, k = r // 2, lax.rem(r, 2)
    ty, tx = t // 2, lax.rem(t, 2)
    rows, query_cols = query_in.shape[0], query_out.shape[1]
    pair_cols = pair_out.shape[2]
    sub = rows // subs
    batch, feats = pieces.shape[1], pieces.shape[2]
    other = [t, ty * 2 + 1 - tx, (1 - ty) * 2 + tx, 3 - t]
    partner = z * 2 + 1 - k

    def piece_id(plane, core, tp):
        return (plane * 2 + core) * 4 + tp

    def part_of(ref, pid, s):
        return ref.at[pl.ds(pl.multiple_of(pid * rows + s * sub, sub), sub)]

    mine = piece_id(z, k, t)

    def columns(tp, first, count):
        return (
            query_in.at[
                pl.ds(first, count), pl.ds(pl.multiple_of(tp * query_cols, query_cols), query_cols)
            ],
            pair_in.at[
                pl.ds(first, count), :, pl.ds(pl.multiple_of(tp * pair_cols, pair_cols), pair_cols)
            ],
        )

    own = columns(t, 0, rows)
    where_own = pl.ds(pl.multiple_of(mine * rows, rows), rows)
    bring = [
        pltpu.make_async_copy(own[0], query_out.at[where_own], local_sem.at[0]),
        pltpu.make_async_copy(own[1], pair_out.at[where_own], local_sem.at[1]),
    ]
    fetch = [
        pltpu.make_async_copy(token_in, token_hold, local_sem.at[2]),
        pltpu.make_async_copy(table_in, table_hold, local_sem.at[3]),
        pltpu.make_async_copy(gain_in, gain_hold, local_sem.at[4]),
        pltpu.make_async_copy(length_in, length_hold, local_sem.at[5]),
        pltpu.make_async_copy(key_in, key_out, local_sem.at[6]),
        pltpu.make_async_copy(value_in, value_out, local_sem.at[7]),
    ]
    for copy in bring:
        copy.start()

    barrier = pltpu.get_barrier_semaphore()
    for j in range(1, 4):
        pl.semaphore_signal(barrier, inc=1, device_id=(r, other[j]), device_id_type=MESH)
    for step in range(1, replicas):
        pl.semaphore_signal(
            barrier, inc=1, device_id=(lax.rem(r + step, replicas), t), device_id_type=MESH
        )
    for copy in fetch[:2]:
        copy.start()
    pl.semaphore_wait(barrier, replicas - 1 + 3)

    def landed(pid, s):
        for c, out in enumerate((query_out, pair_out)):
            place = part_of(out, pid, s)
            pltpu.make_async_copy(place, place, recv_sem.at[c, pid * subs + s]).wait()

    def copies(pid, s, way, slot, target):
        return [
            pltpu.make_async_remote_copy(
                src_ref=part_of(out, pid, s),
                dst_ref=part_of(out, pid, s),
                send_sem=send_sem.at[c, way, slot * subs + s],
                recv_sem=recv_sem.at[c, pid * subs + s],
                device_id=target,
                device_id_type=MESH,
            )
            for c, out in enumerate((query_out, pair_out))
        ]

    def across(j, s):
        return [
            pltpu.make_async_remote_copy(
                src_ref=source,
                dst_ref=part_of(out, mine, s),
                send_sem=across_sem.at[c, (j - 1) * subs + s],
                recv_sem=recv_sem.at[c, mine * subs + s],
                device_id=(r, other[j]),
                device_id_type=MESH,
            )
            for c, (source, out) in enumerate(
                zip(
                    columns(other[j], pl.multiple_of(s * sub, sub), sub),
                    (query_out, pair_out),
                )
            )
        ]

    def onward(pid, s, slot, up, down, wait=False):
        def act(made):
            for copy in made:
                copy.wait_send() if wait else copy.start()

        if up:

            @pl.when(z < planes - 1)
            def _():
                act(copies(pid, s, 0, slot, (lax.rem(r + 2, replicas), t)))

        if down:

            @pl.when(z > 0)
            def _():
                act(copies(pid, s, 1, slot, (lax.rem(r + replicas - 2, replicas), t)))

        act(copies(pid, s, 2, slot, (partner, t)))

    def each_sub(act):
        def body(s, carry):
            act(s)
            return carry

        lax.fori_loop(0, subs, body, 0)

    def near(j, wait=False):
        pid = piece_id(z, k, other[j])

        def act(s):
            if not wait and j > 0:
                landed(pid, s)
            onward(pid, s, j, True, True, wait)

        each_sub(act)

    def far_away(far, j, wait=False):
        @pl.when(z >= far)
        def _():
            pid = piece_id(lax.rem(z + planes - far, planes), k, other[j])

            def act(s):
                if not wait:
                    landed(pid, s)
                onward(pid, s, 4 * far + j, True, False, wait)

            each_sub(act)

        @pl.when(z + far < planes)
        def _():
            pid = piece_id(lax.rem(z + far, planes), k, other[j])

            def act(s):
                if not wait:
                    landed(pid, s)
                onward(pid, s, 4 * (planes - 1 + far) + j, False, True, wait)

            each_sub(act)

    for copy in bring:
        copy.wait()

    def send_across(s):
        for j in range(1, 4):
            for copy in across(j, s):
                copy.start()

    near(0)
    each_sub(send_across)
    for copy in fetch[2:]:
        copy.start()

    gives = [
        pltpu.make_async_remote_copy(
            src_ref=part_ref.at[plane, 1 - k],
            dst_ref=given.at[plane],
            send_sem=give_send.at[plane],
            recv_sem=give_recv.at[plane],
            device_id=(partner, t),
            device_id_type=MESH,
        )
        for plane in range(planes)
    ]

    last = planes - 1

    def picks(dest, wait=None):
        stop = 1 if dest == 0 else last - 1 if dest == last else dest
        table, send, recv = (
            (picked, pick_send, pick_recv)
            if stop == dest
            else (relayed, relay_send, relay_recv)
        )

        @pl.when((z != dest) & (z != stop))
        def _():
            copy = pltpu.make_async_remote_copy(
                src_ref=joined.at[dest],
                dst_ref=table.at[z],
                send_sem=send.at[dest],
                recv_sem=recv.at[z],
                device_id=(stop * 2 + k, t),
                device_id_type=MESH,
            )
            copy.wait_send() if wait else copy.start()

    def arrived(table, recv, source):
        place = table.at[source]
        pltpu.make_async_copy(place, place, recv.at[source]).wait()

    def relay(dest):
        stop = 1 if dest == 0 else last - 1
        return pltpu.make_async_remote_copy(
            src_ref=relay_sum,
            dst_ref=relay_in,
            send_sem=relay_send.at[planes],
            recv_sem=relay_recv.at[planes],
            device_id=(dest * 2 + k, t),
            device_id_type=MESH,
        ), stop

    gather = [
        pltpu.make_async_remote_copy(
            src_ref=pieces.at[t],
            dst_ref=pieces.at[t],
            send_sem=piece_send.at[j - 1],
            recv_sem=piece_recv.at[j - 1],
            device_id=(r, other[j]),
            device_id_type=MESH,
        )
        for j in range(1, 4)
    ]

    def select_rows():
        fetch[0].wait()
        vocab_rows = table_hold.shape[0]
        tokens = token_hold.shape[1]
        lanes = 128
        wanted = jnp.broadcast_to(token_hold[...] - r * vocab_rows, (lanes, tokens)).T
        lane = lax.broadcasted_iota(jnp.int32, (tokens, lanes), 1)
        for first in range(0, vocab_rows, lanes):
            onehot_ref[:, first : first + lanes] = (wanted == lane + first).astype(
                onehot_ref.dtype
            )
        fetch[1].wait()
        block = 256

        def select(i, carry):
            where = pl.ds(pl.multiple_of(i * block, block), block)
            rows_here = jnp.dot(
                onehot_ref[...], table_hold[:, where], preferred_element_type=jnp.float32
            ).astype(jnp.bfloat16)
            part_ref[:, :, :, where] = rows_here.reshape(planes, 2, batch, block)
            return carry

        lax.fori_loop(0, feats // block, select, 0)

    def join():
        for copy in gives:
            copy.wait()
        for plane in range(planes):
            kept = part_ref[plane, k].astype(jnp.float32)
            joined[plane] = (kept + given[plane].astype(jnp.float32)).astype(jnp.bfloat16)

    def pass_on():
        for dest in (0, last):
            copy, stop = relay(dest)

            @pl.when(z == stop)
            def _():
                total = joined[dest].astype(jnp.float32)
                for source in range(planes):
                    if source not in (dest, stop):
                        arrived(relayed, relay_recv, source)
                        total = total + relayed[source].astype(jnp.float32)
                relay_sum[...] = total.astype(jnp.bfloat16)
                copy.start()

    def sum_picks():
        for dest in range(planes):

            @pl.when(z == dest)
            def _():
                total = joined[dest].astype(jnp.float32)
                if dest in (0, last):
                    relay(dest)[0].wait_recv()
                    total = total + relay_in[...].astype(jnp.float32)
                else:
                    for source in range(planes):
                        if source != dest:
                            arrived(picked, pick_recv, source)
                            total = total + picked[source].astype(jnp.float32)
                pieces[t] = total.astype(jnp.bfloat16)

    def normalise():
        fetch[2].wait()
        gain_wide[...] = gain_hold[...].astype(jnp.float32)
        for copy in gather:
            copy.wait()
        square = jnp.zeros((batch, 1), jnp.float32)
        for i in range(4):
            part = pieces[i].astype(jnp.float32)
            square = square + jnp.sum(part * part, axis=1, keepdims=True)
        factor = lax.rsqrt(square / (4 * feats) + 1e-05)
        lanes = gain_wide.shape[1]
        blocks = feats // lanes
        for i in range(4):

            def scaled(b, carry):
                part = pieces[i, :, pl.ds(pl.multiple_of(b * lanes, lanes), lanes)]
                gain = gain_wide[pl.ds(i * blocks + b, 1), :]
                where = pl.ds(pl.multiple_of(i * feats + b * lanes, lanes), lanes)
                normed_ref[:, where] = (part.astype(jnp.float32) * factor * gain).astype(
                    jnp.bfloat16
                )
                return carry

            lax.fori_loop(0, blocks, scaled, 0)
        block = 256
        line = lax.broadcasted_iota(jnp.int32, (block, 2 * block), 0)
        column = lax.broadcasted_iota(jnp.int32, (block, 2 * block), 1)
        even = (column == 2 * line).astype(jnp.bfloat16)
        odd = (column == 2 * line + 1).astype(jnp.bfloat16)

        def spread(i, carry):
            part = normed_ref[:, pl.ds(pl.multiple_of(i * block, block), block)]
            where = pl.ds(pl.multiple_of(i * 2 * block, 2 * block), 2 * block)
            spread_ref[0:batch, where] = jnp.dot(
                part, even, preferred_element_type=jnp.float32
            ).astype(jnp.bfloat16)
            spread_ref[batch : 2 * batch, where] = jnp.dot(
                part, odd, preferred_element_type=jnp.float32
            ).astype(jnp.bfloat16)
            return carry

        lax.fori_loop(0, 4 * feats // block, spread, 0)

    def lengths():
        fetch[3].wait()
        group = length_out.shape[1]
        for s in range(batch):
            length_out[s] = jnp.full((group, length_out.shape[2]), length_hold[s], jnp.int32)

    select_rows()
    for copy in gives:
        copy.start()
    join()
    for dest in range(planes):
        picks(dest)
    near(1)
    near(2)
    far_away(1, 0)
    near(3)
    pass_on()
    far_away(1, 1)
    far_away(1, 2)
    sum_picks()
    for copy in gather:
        copy.start()
    far_away(1, 3)
    normalise()
    lengths()
    for far in range(2, planes):
        for j in range(4):
            far_away(far, j)

    for copy in fetch[4:]:
        copy.wait()

    def sent_across(s):
        for j in range(1, 4):
            for copy in across(j, s):
                copy.wait_send()

    each_sub(sent_across)
    for dest in range(planes):
        picks(dest, wait=True)
    for dest in (0, last):
        copy, stop = relay(dest)

        @pl.when(z == stop)
        def _():
            copy.wait_send()

    for j in range(4):
        near(j, wait=True)
    for far in range(1, planes):
        for j in range(4):
            far_away(far, j, wait=True)
    for plane in range(planes):
        for j in range(4):
            pid = piece_id(plane, 1 - k, j)
            each_sub(functools.partial(landed, pid))


def exchange(
    token_ids, norm_gain, embed_table, w_query, w_keyvalue, key_cache, value_cache, lengths, planes
):
    rows, all_query = w_query.shape
    query_cols, pair_cols = all_query // 4, w_keyvalue.shape[2] // 4
    replicas = 2 * planes
    width = rows * replicas * 4
    feats = embed_table.shape[1]
    kind = w_query.dtype
    batch, head_size = lengths.shape[0], key_cache.shape[2]
    group = query_cols // head_size
    tokens = token_ids.shape[0]
    lanes = 128
    subs = 2
    anywhere = pl.BlockSpec(memory_space=pl.ANY)
    vmem = pl.BlockSpec(memory_space=pltpu.VMEM)
    dma = pltpu.SemaphoreType.DMA
    slots = 4 * (2 * planes - 1) * subs
    shape = jax.ShapeDtypeStruct
    return pl.pallas_call(
        functools.partial(exchange_kernel, planes, subs),
        out_shape=(
            pltpu.VMEM((width, query_cols), kind),
            pltpu.VMEM((width, 2, pair_cols), kind),
            pltpu.VMEM(key_cache.shape, kind),
            pltpu.VMEM(value_cache.shape, kind),
            pltpu.VMEM((batch, group, head_size), jnp.int32),
            pltpu.VMEM((batch, width), kind),
            pltpu.VMEM((2 * batch, 2 * width), kind),
        ),
        in_specs=[anywhere] * 8,
        out_specs=(vmem,) * 7,
        scratch_shapes=[
            pltpu.VMEM((1, tokens), jnp.int32),
            pltpu.VMEM((width // lanes, lanes), kind),
            pltpu.VMEM((width // lanes, lanes), jnp.float32),
            pltpu.SMEM((batch,), jnp.int32),
            pltpu.VMEM(embed_table.shape, kind),
            pltpu.VMEM((tokens, embed_table.shape[0]), kind),
            pltpu.VMEM((planes, 2, batch, feats), kind),
            pltpu.VMEM((planes, batch, feats), kind),
            pltpu.VMEM((planes, batch, feats), kind),
            pltpu.VMEM((planes, batch, feats), kind),
            pltpu.VMEM((planes, batch, feats), kind),
            pltpu.VMEM((batch, feats), kind),
            pltpu.VMEM((batch, feats), kind),
            pltpu.VMEM((4, batch, feats), kind),
            dma((2, 3, slots)),
            dma((2, replicas * 4 * subs)),
            dma((2, 3 * subs)),
            dma((8,)),
            dma((planes,)),
            dma((planes,)),
            dma((planes,)),
            dma((planes,)),
            dma((planes + 1,)),
            dma((planes + 1,)),
            dma((3,)),
            dma((3,)),
        ],
        compiler_params=pltpu.CompilerParams(
            collective_id=0, has_side_effects=True, vmem_limit_bytes=8 * 2**20
        ),
        cost_estimate=pl.CostEstimate(
            flops=2 * 10**11, bytes_accessed=2 * width * query_cols, transcendentals=0
        ),
        name="weight_exchange",
    )(
        *(
            pltpu.with_memory_space_constraint(operand, pltpu.HBM)
            for operand in (
                token_ids.reshape(1, tokens),
                norm_gain.reshape(-1, lanes),
                lengths,
                embed_table,
                w_query,
                w_keyvalue,
                key_cache,
                value_cache,
            )
        )
    )


def finish_kernel(
    normed_ref,
    spread_ref,
    query_all,
    pair_all,
    key_ref,
    value_ref,
    length_ref,
    query_ref,
    pair_ref,
    context_ref,
    query_heads,
    context_heads,
    sems,
):
    batch, width = normed_ref.shape
    query_cols, pair_cols = query_all.shape[1], pair_all.shape[1]
    group, head_size = query_heads.shape[1], query_heads.shape[2]
    parts = sems.shape[1]
    stores = []
    for c, (held, out) in enumerate(((query_all, query_ref), (pair_all, pair_ref))):
        size = held.shape[0] // parts
        for i in range(parts):
            where = pl.ds(i * size, size)
            stores.append(pltpu.make_async_copy(held.at[where], out.at[where], sems.at[c, i]))
    for copy in stores:
        copy.start()

    block = 512

    def project(i, carry):
        query, pair = carry
        here = pl.ds(pl.multiple_of(i * block, block), block)
        twice = pl.ds(pl.multiple_of(i * 2 * block, 2 * block), 2 * block)
        query = query + jnp.dot(
            normed_ref[:, here], query_all[here, :], preferred_element_type=jnp.float32
        )
        pair = pair + jnp.dot(
            spread_ref[:, twice], pair_all[twice, :], preferred_element_type=jnp.float32
        )
        return query, pair

    query, pair = lax.fori_loop(
        0,
        width // block,
        project,
        (
            jnp.zeros((batch, query_cols), jnp.float32),
            jnp.zeros((2 * batch, pair_cols), jnp.float32),
        ),
    )
    query = query.astype(jnp.bfloat16).astype(jnp.float32)
    pair = pair.astype(jnp.bfloat16).astype(jnp.float32)
    for j in range(group):
        query_heads[:, j, :] = query[:, j * head_size : (j + 1) * head_size]

    scale = head_size ** (-0.5)
    slots = key_ref.shape[1]
    position = lax.broadcasted_iota(jnp.int32, (group, slots), 1)
    for s in range(batch):
        heads = query_heads[s]
        scores = (
            lax.dot_general(
                heads.astype(jnp.bfloat16),
                key_ref[s],
                (((1,), (1,)), ((), ())),
                preferred_element_type=jnp.float32,
            )
            * scale
        )
        scores = jnp.where(position < length_ref[s, :, 0:1], scores, -jnp.inf)
        own = jnp.sum(heads * pair[s : s + 1], axis=1, keepdims=True) * scale
        top = jnp.maximum(jnp.max(scores, axis=1, keepdims=True), own)
        weights = jnp.exp(scores - top)
        own_weight = jnp.exp(own - top)
        total = jnp.sum(weights, axis=1, keepdims=True) + own_weight
        weights = (weights / total).astype(jnp.bfloat16)
        own_weight = (own_weight / total).astype(jnp.bfloat16).astype(jnp.float32)
        context = jnp.dot(weights, value_ref[s], preferred_element_type=jnp.float32)
        context_heads[s] = context + own_weight * pair[batch + s : batch + s + 1]
    for j in range(group):
        context_ref[:, j * head_size : (j + 1) * head_size] = context_heads[:, j, :].astype(
            context_ref.dtype
        )
    for copy in stores:
        copy.wait()


def finish(normed, spread, query_all, pair_all, keys, values, lengths):
    batch, width = normed.shape
    query_cols, pair_cols = query_all.shape[1], pair_all.shape[2]
    head_size = keys.shape[2]
    group = query_cols // head_size
    pair_flat = pair_all.reshape(2 * width, pair_cols)
    anywhere = pl.BlockSpec(memory_space=pl.ANY)
    vmem = pl.BlockSpec(memory_space=pltpu.VMEM)
    shape = jax.ShapeDtypeStruct
    query_out, pair_out, context = pl.pallas_call(
        finish_kernel,
        out_shape=(
            shape(query_all.shape, query_all.dtype),
            shape(pair_flat.shape, pair_all.dtype),
            shape((batch, query_cols), normed.dtype),
        ),
        in_specs=[vmem] * 7,
        out_specs=(
            pl.BlockSpec(memory_space=pltpu.HBM),
            pl.BlockSpec(memory_space=pltpu.HBM),
            vmem,
        ),
        scratch_shapes=[
            pltpu.VMEM((batch, group, head_size), jnp.float32),
            pltpu.VMEM((batch, group, head_size), jnp.float32),
            pltpu.SemaphoreType.DMA((2, 4)),
        ],
        compiler_params=pltpu.CompilerParams(vmem_limit_bytes=8 * 2**20),
        cost_estimate=pl.CostEstimate(
            flops=2 * batch * width * (query_cols + 4 * pair_cols),
            bytes_accessed=4 * width * (query_cols + 2 * pair_cols),
            transcendentals=0,
        ),
        name="project_attend_store",
    )(normed, spread, query_all, pair_flat, keys, values, lengths)
    return context, query_out, pair_out.reshape(width, 2, pair_cols)


def per_device_line(
    planes,
    token_ids,
    embed_table,
    norm_gain,
    w_query,
    w_keyvalue,
    key_cache,
    value_cache,
    cache_lengths,
):
    query_all, pair_all, keys, values, lengths, normed, spread = exchange(
        token_ids,
        norm_gain,
        embed_table,
        w_query,
        w_keyvalue,
        key_cache,
        value_cache,
        cache_lengths,
        planes,
    )
    return finish(normed, spread, query_all, pair_all, keys, values, lengths)


def solution(mesh):
    replicas, tp = mesh.shape["replica"], mesh.shape["tp"]

    def body(*args):
        key_cache, lengths, w_keyvalue = args[5], args[7], args[4]
        one_head = w_keyvalue.shape[2] == tp * key_cache.shape[2]
        own_rows = key_cache.shape[0] == lengths.shape[0]
        if tp == 4 and replicas % 2 == 0 and replicas > 6 and one_head and own_rows:
            return per_device_line(replicas // 2, *args)
        return per_device(*args)

    return jax.shard_map(
        body,
        mesh=mesh,
        in_specs=(
            P(),
            P("replica", "tp"),
            P(),
            P(("replica", "tp"), None),
            P(("replica", "tp"), None, None),
            P(("replica", "tp"), None, None),
            P(("replica", "tp"), None, None),
            P("replica"),
        ),
        out_specs=(P(("replica", "tp"), None), P(None, "tp"), P(None, None, "tp")),
        check_vma=False,
    )
```

time: 205 us -> 197 us (0.961)
  local copies, waits for them, and re-layouts: 7.45 us -> 0 us
  Pallas kernels: 193 us -> 196 us
  matrix products: 2.12 us -> 0 us
    unnamed x14 -> x0, local copies, waits for them, and re-layouts: 5.95 us -> none
    pallas_call x2, Pallas kernels: 193 us -> 196 us  [the longest x1 185 us: exchange(): pl.pallas_call(functools.partial(exchange_kernel, planes, subs), out_shap...]
    dot_general x3 -> x0, matrix products: 2.12 us -> none  [the longest x1 1.27 us: attend(): jnp.einsum('rgd,rcd->rgc', query, keys, preferred_element_type=jnp.float32)]
where the time goes in v1:
time: 197 us
  Pallas kernels  196 us (99%)
    pallas_call x1, Pallas kernels, exchange(): pl.pallas_call(functools.partial(exchange_kernel, planes, subs), out_shap...  185 us
    pallas_call x1, Pallas kernels, finish(): pl.pallas_call(finish_kernel, out_shape=(shape(query_all.shape, query_all...  11.7 us

profile of v1, /device:TPU:1, one launch (start us, length us, event | category | flops | bytes accessed | tf_op | source)
XLA Modules:
  0.0 196.9 jit_solution(12193882260234821776)
XLA Ops:
  0.6 184.6 %weight_exchange.1 = (bf16[8192,1024]{1,0:T(8,128)(2,1)S(1)}, bf16[8192,2,128]{2,1,0:T(2,128)(2,1)S(1)}, bf16[16,1024,128]{2,1,0:T(8,128)(2,1)S(1)}, bf16[16,102...) custom-call(s32[1,128]{1,0:T(1,128)} %bitcast.7, ...), custom_call_target="tpu_custom_call" | custom-call | flops 199999995904 | bytes 16777216 | tf_op jit(solution)/shard_map/weight_exchange/pallas_call | solution.py:563
  185.2 11.7 %project_attend_store.1 = (bf16[8192,1024]{1,0:T(8,128)(2,1)}, bf16[16384,128]{1,0:T(8,128)(2,1)}, bf16[16,1024]{1,0:T(8,128)(2,1)}) custom-call(bf16[16,8192]{1,0:T(8,128)(2,1)S(1)} %get-tuple-element.13.normed_ref, bf16[32,16384]{1,0:T(8,128)(2,1)S(1)} %get-tuple-element.14.spread_ref, bf16[8192,1024]{1,0:T(8,128)(2,1)S(1)} %get-tuple-element.15.query_all, ...), custom_call_target="tpu_custom_call" | custom-call | flops 402653184 | bytes 41943040 | tf_op jit(solution)/shard_map/project_attend_store/pallas_call | solution.py:725

commit v2 on v1

--- a/solution.py
+++ b/solution.py
@@ -126,6 +126,7 @@
     length_out,
     normed_ref,
     spread_ref,
+    query_acc,
     token_hold,
     gain_hold,
     gain_wide,
@@ -135,21 +136,18 @@
     part_ref,
     given,
     joined,
-    picked,
-    relayed,
-    relay_sum,
-    relay_in,
+    sums,
+    brought,
     pieces,
     send_sem,
     recv_sem,
+    hand_recv,
     across_sem,
     local_sem,
     give_send,
     give_recv,
-    pick_send,
-    pick_recv,
-    relay_send,
-    relay_recv,
+    sum_send,
+    sum_recv,
     piece_send,
     piece_recv,
 ):
@@ -202,38 +200,53 @@
     barrier = pltpu.get_barrier_semaphore()
     for j in range(1, 4):
         pl.semaphore_signal(barrier, inc=1, device_id=(r, other[j]), device_id_type=MESH)
-    for step in range(1, replicas):
-        pl.semaphore_signal(
-            barrier, inc=1, device_id=(lax.rem(r + step, replicas), t), device_id_type=MESH
-        )
+    pl.semaphore_signal(barrier, inc=1, device_id=(partner, t), device_id_type=MESH)
+    above, below = lax.rem(r + 2, replicas), lax.rem(r + replicas - 2, replicas)
+
+    @pl.when(z < planes - 1)
+    def _():
+        pl.semaphore_signal(barrier, inc=1, device_id=(above, t), device_id_type=MESH)
+
+    @pl.when(z > 0)
+    def _():
+        pl.semaphore_signal(barrier, inc=1, device_id=(below, t), device_id_type=MESH)
+
     for copy in fetch[:2]:
         copy.start()
-    pl.semaphore_wait(barrier, replicas - 1 + 3)
+    pl.semaphore_wait(barrier, 4 + jnp.minimum(z, 1) + jnp.minimum(planes - 1 - z, 1))
 
     def landed(pid, s):
         for c, out in enumerate((query_out, pair_out)):
             place = part_of(out, pid, s)
             pltpu.make_async_copy(place, place, recv_sem.at[c, pid * subs + s]).wait()
 
-    def copies(pid, s, way, slot, target):
-        return [
+    def send(pid, s, way, target):
+        for c, out in enumerate((query_out, pair_out)):
             pltpu.make_async_remote_copy(
                 src_ref=part_of(out, pid, s),
                 dst_ref=part_of(out, pid, s),
-                send_sem=send_sem.at[c, way, slot * subs + s],
-                recv_sem=recv_sem.at[c, pid * subs + s],
+                send_sem=send_sem.at[c, way],
+                recv_sem=hand_recv.at[c, pid] if way == 2 else recv_sem.at[c, pid * subs + s],
                 device_id=target,
                 device_id_type=MESH,
-            )
-            for c, out in enumerate((query_out, pair_out))
-        ]
+            ).start()
+
+    def sent(way, pieces_sent):
+        for c, out in enumerate((query_out, pair_out)):
+            place = out.at[0 : pieces_sent * rows]
+            pltpu.make_async_copy(place, place, send_sem.at[c, way]).wait()
+
+    def handed(pid):
+        for c, out in enumerate((query_out, pair_out)):
+            place = out.at[pl.ds(pl.multiple_of(pid * rows, rows), rows)]
+            pltpu.make_async_copy(place, place, hand_recv.at[c, pid]).wait()
 
     def across(j, s):
         return [
             pltpu.make_async_remote_copy(
                 src_ref=source,
                 dst_ref=part_of(out, mine, s),
-                send_sem=across_sem.at[c, (j - 1) * subs + s],
+                send_sem=across_sem.at[c],
                 recv_sem=recv_sem.at[c, mine * subs + s],
                 device_id=(r, other[j]),
                 device_id_type=MESH,
@@ -246,24 +259,20 @@
             )
         ]
 
-    def onward(pid, s, slot, up, down, wait=False):
-        def act(made):
-            for copy in made:
-                copy.wait_send() if wait else copy.start()
-
+    def onward(pid, s, up, down):
         if up:
 
             @pl.when(z < planes - 1)
             def _():
-                act(copies(pid, s, 0, slot, (lax.rem(r + 2, replicas), t)))
+                send(pid, s, 0, (above, t))
 
         if down:
 
             @pl.when(z > 0)
             def _():
-                act(copies(pid, s, 1, slot, (lax.rem(r + replicas - 2, replicas), t)))
-
-        act(copies(pid, s, 2, slot, (partner, t)))
+                send(pid, s, 1, (below, t))
+
+        send(pid, s, 2, (partner, t))
 
     def each_sub(act):
         def body(s, carry):
@@ -272,49 +281,70 @@
 
         lax.fori_loop(0, subs, body, 0)
 
-    def near(j, wait=False):
+    def near(j):
         pid = piece_id(z, k, other[j])
 
         def act(s):
-            if not wait and j > 0:
+            if j > 0:
                 landed(pid, s)
-            onward(pid, s, j, True, True, wait)
+            onward(pid, s, True, True)
 
         each_sub(act)
 
-    def far_away(far, j, wait=False):
+    def planes_at(far, act):
+        if far == 0:
+            act(z, True)
+            return
+
         @pl.when(z >= far)
         def _():
-            pid = piece_id(lax.rem(z + planes - far, planes), k, other[j])
-
-            def act(s):
-                if not wait:
-                    landed(pid, s)
-                onward(pid, s, 4 * far + j, True, False, wait)
-
-            each_sub(act)
+            act(lax.rem(z + planes - far, planes), True)
 
         @pl.when(z + far < planes)
         def _():
-            pid = piece_id(lax.rem(z + far, planes), k, other[j])
+            act(lax.rem(z + far, planes), False)
+
+    def far_away(far, j):
+        def forward(plane, up):
+            pid = piece_id(plane, k, other[j])
 
             def act(s):
-                if not wait:
-                    landed(pid, s)
-                onward(pid, s, 4 * (planes - 1 + far) + j, False, True, wait)
+                landed(pid, s)
+                onward(pid, s, up, not up)
 
             each_sub(act)
+
+        planes_at(far, forward)
+
+    def multiply(far, j):
+        def both(plane, up):
+            handed(piece_id(plane, 1 - k, other[j]))
+
+            def add(core, carry):
+                pid = piece_id(plane, core, other[j])
+                where = pl.ds(pl.multiple_of(pid * rows, rows), rows)
+                query_acc[...] += jnp.dot(
+                    normed_ref[:, where], query_out[where, :], preferred_element_type=jnp.float32
+                )
+                return carry
+
+            lax.fori_loop(0, 2, add, 0)
+
+        planes_at(far, both)
 
     for copy in bring:
         copy.wait()
 
-    def send_across(s):
-        for j in range(1, 4):
+    def send_across(j):
+        def act(s):
             for copy in across(j, s):
                 copy.start()
 
+        each_sub(act)
+
     near(0)
-    each_sub(send_across)
+    for j in range(1, 4):
+        send_across(j)
     for copy in fetch[2:]:
         copy.start()
 
@@ -332,40 +362,37 @@
 
     last = planes - 1
 
-    def picks(dest, wait=None):
-        stop = 1 if dest == 0 else last - 1 if dest == last else dest
-        table, send, recv = (
-            (picked, pick_send, pick_recv)
-            if stop == dest
-            else (relayed, relay_send, relay_recv)
-        )
-
-        @pl.when((z != dest) & (z != stop))
-        def _():
-            copy = pltpu.make_async_remote_copy(
-                src_ref=joined.at[dest],
-                dst_ref=table.at[z],
-                send_sem=send.at[dest],
-                recv_sem=recv.at[z],
-                device_id=(stop * 2 + k, t),
-                device_id_type=MESH,
-            )
-            copy.wait_send() if wait else copy.start()
-
-    def arrived(table, recv, source):
-        place = table.at[source]
-        pltpu.make_async_copy(place, place, recv.at[source]).wait()
-
-    def relay(dest):
-        stop = 1 if dest == 0 else last - 1
-        return pltpu.make_async_remote_copy(
-            src_ref=relay_sum,
-            dst_ref=relay_in,
-            send_sem=relay_send.at[planes],
-            recv_sem=relay_recv.at[planes],
-            device_id=(dest * 2 + k, t),
-            device_id_type=MESH,
-        ), stop
+    def passing(hop, wait=False):
+        for way in range(2):
+            for plane in range(planes - 1):
+                if plane != hop and not wait:
+                    continue
+                place = plane if way == 0 else last - plane
+                target = (place + 1 if way == 0 else place - 1) * 2 + k
+                dests = range(place + 1, planes) if way == 0 else range(place)
+
+                @pl.when(z == place)
+                def _():
+                    for dest in dests:
+                        if plane > 0 and not wait:
+                            came(way, dest)
+                            total = joined[dest].astype(jnp.float32) + brought[
+                                way, dest
+                            ].astype(jnp.float32)
+                            sums[way, dest] = total.astype(jnp.bfloat16)
+                        copy = pltpu.make_async_remote_copy(
+                            src_ref=sums.at[way, dest] if plane > 0 else joined.at[dest],
+                            dst_ref=brought.at[way, dest],
+                            send_sem=sum_send.at[way, dest],
+                            recv_sem=sum_recv.at[way, dest],
+                            device_id=(target, t),
+                            device_id_type=MESH,
+                        )
+                        copy.wait_send() if wait else copy.start()
+
+    def came(way, dest):
+        place = brought.at[way, dest]
+        pltpu.make_async_copy(place, place, sum_recv.at[way, dest]).wait()
 
     gather = [
         pltpu.make_async_remote_copy(
@@ -410,34 +437,16 @@
             kept = part_ref[plane, k].astype(jnp.float32)
             joined[plane] = (kept + given[plane].astype(jnp.float32)).astype(jnp.bfloat16)
 
-    def pass_on():
-        for dest in (0, last):
-            copy, stop = relay(dest)
-
-            @pl.when(z == stop)
-            def _():
-                total = joined[dest].astype(jnp.float32)
-                for source in range(planes):
-                    if source not in (dest, stop):
-                        arrived(relayed, relay_recv, source)
-                        total = total + relayed[source].astype(jnp.float32)
-                relay_sum[...] = total.astype(jnp.bfloat16)
-                copy.start()
-
-    def sum_picks():
+    def sum_all():
         for dest in range(planes):
 
             @pl.when(z == dest)
             def _():
                 total = joined[dest].astype(jnp.float32)
-                if dest in (0, last):
-                    relay(dest)[0].wait_recv()
-                    total = total + relay_in[...].astype(jnp.float32)
-                else:
-                    for source in range(planes):
-                        if source != dest:
-                            arrived(picked, pick_recv, source)
-                            total = total + picked[source].astype(jnp.float32)
+                for way in range(2):
+                    if dest != (0 if way == 0 else last):
+                        came(way, dest)
+                        total = total + brought[way, dest].astype(jnp.float32)
                 pieces[t] = total.astype(jnp.bfloat16)
 
     def normalise():
@@ -493,52 +502,46 @@
     for copy in gives:
         copy.start()
     join()
-    for dest in range(planes):
-        picks(dest)
-    near(1)
-    near(2)
-    far_away(1, 0)
-    near(3)
-    pass_on()
-    far_away(1, 1)
-    far_away(1, 2)
-    sum_picks()
-    for copy in gather:
-        copy.start()
-    far_away(1, 3)
-    normalise()
-    lengths()
-    for far in range(2, planes):
-        for j in range(4):
-            far_away(far, j)
+    passing(0)
+    order = [(0, 1), (0, 2), (1, 0), (0, 3)]
+    order += [(far, j) for far in range(1, planes) for j in range(4) if (far, j) != (1, 0)]
+    middle = len(order) - 5
+    for step, (far, j) in enumerate(order):
+        near(j) if far == 0 else far_away(far, j)
+        if step == 1:
+            passing(1)
+        if step > 4 and step - 3 < planes - 1:
+            passing(step - 3)
+        if step == middle - 1:
+            sum_all()
+            for copy in gather:
+                copy.start()
+        if step == middle:
+            normalise()
+            lengths()
+            query_acc[...] = jnp.zeros_like(query_acc)
+            for past in [(0, 0)] + order[:middle]:
+                multiply(*past)
+        if step > middle:
+            multiply(*order[step - 1])
 
     for copy in fetch[4:]:
         copy.wait()
-
-    def sent_across(s):
-        for j in range(1, 4):
-            for copy in across(j, s):
-                copy.wait_send()
-
-    each_sub(sent_across)
-    for dest in range(planes):
-        picks(dest, wait=True)
-    for dest in (0, last):
-        copy, stop = relay(dest)
-
-        @pl.when(z == stop)
+    for c, out in enumerate((query_out, pair_out)):
+        place = out.at[0 : 3 * rows]
+        pltpu.make_async_copy(place, place, across_sem.at[c]).wait()
+    passing(0, wait=True)
+    multiply(*order[-1])
+    for place in range(planes):
+
+        @pl.when(z == place)
         def _():
-            copy.wait_send()
-
-    for j in range(4):
-        near(j, wait=True)
-    for far in range(1, planes):
-        for j in range(4):
-            far_away(far, j, wait=True)
-    for plane in range(planes):
-        for j in range(4):
-            pid = piece_id(plane, 1 - k, j)
-            each_sub(functools.partial(landed, pid))
+            if place < last:
+                sent(0, 4 * (place + 1))
+            if place > 0:
+                sent(1, 4 * (planes - place))
+
+    sent(2, 4 * planes)
 
 
 def exchange(
@@ -558,7 +561,6 @@
     anywhere = pl.BlockSpec(memory_space=pl.ANY)
     vmem = pl.BlockSpec(memory_space=pltpu.VMEM)
     dma = pltpu.SemaphoreType.DMA
-    slots = 4 * (2 * planes - 1) * subs
     shape = jax.ShapeDtypeStruct
     return pl.pallas_call(
         functools.partial(exchange_kernel, planes, subs),
@@ -570,9 +572,10 @@
             pltpu.VMEM((batch, group, head_size), jnp.int32),
             pltpu.VMEM((batch, width), kind),
             pltpu.VMEM((2 * batch, 2 * width), kind),
+            pltpu.VMEM((batch, query_cols), jnp.float32),
         ),
         in_specs=[anywhere] * 8,
-        out_specs=(vmem,) * 7,
+        out_specs=(vmem,) * 8,
         scratch_shapes=[
             pltpu.VMEM((1, tokens), jnp.int32),
             pltpu.VMEM((width // lanes, lanes), kind),
@@ -583,21 +586,18 @@
             pltpu.VMEM((planes, 2, batch, feats), kind),
             pltpu.VMEM((planes, batch, feats), kind),
             pltpu.VMEM((planes, batch, feats), kind),
-            pltpu.VMEM((planes, batch, feats), kind),
-            pltpu.VMEM((planes, batch, feats), kind),
-            pltpu.VMEM((batch, feats), kind),
-            pltpu.VMEM((batch, feats), kind),
+            pltpu.VMEM((2, planes, batch, feats), kind),
+            pltpu.VMEM((2, planes, batch, feats), kind),
             pltpu.VMEM((4, batch, feats), kind),
-            dma((2, 3, slots)),
+            dma((2, 3)),
             dma((2, replicas * 4 * subs)),
-            dma((2, 3 * subs)),
+            dma((2, replicas * 4)),
+            dma((2,)),
             dma((8,)),
             dma((planes,)),
             dma((planes,)),
-            dma((planes,)),
-            dma((planes,)),
-            dma((planes + 1,)),
-            dma((planes + 1,)),
+            dma((2, planes)),
+            dma((2, planes)),
             dma((3,)),
             dma((3,)),
         ],
@@ -626,7 +626,7 @@
 
 
 def finish_kernel(
-    normed_ref,
+    query_acc,
     spread_ref,
     query_all,
     pair_all,
@@ -637,12 +637,15 @@
     pair_ref,
     context_ref,
     query_heads,
+    scores_ref,
+    weights_ref,
     context_heads,
+    context_hold,
     sems,
+    context_sem,
 ):
-    batch, width = normed_ref.shape
-    query_cols, pair_cols = query_all.shape[1], pair_all.shape[1]
-    group, head_size = query_heads.shape[1], query_heads.shape[2]
+    pair_cols = pair_all.shape[1]
+    batch, group, head_size = query_heads.shape
     parts = sems.shape[1]
     stores = []
     for c, (held, out) in enumerate(((query_all, query_ref), (pair_all, pair_ref))):
@@ -653,101 +656,97 @@
     for copy in stores:
         copy.start()
 
-    block = 512
-
-    def project(i, carry):
-        query, pair = carry
-        here = pl.ds(pl.multiple_of(i * block, block), block)
-        twice = pl.ds(pl.multiple_of(i * 2 * block, 2 * block), 2 * block)
-        query = query + jnp.dot(
-            normed_ref[:, here], query_all[here, :], preferred_element_type=jnp.float32
-        )
-        pair = pair + jnp.dot(
-            spread_ref[:, twice], pair_all[twice, :], preferred_element_type=jnp.float32
-        )
-        return query, pair
-
-    query, pair = lax.fori_loop(
-        0,
-        width // block,
-        project,
-        (
-            jnp.zeros((batch, query_cols), jnp.float32),
-            jnp.zeros((2 * batch, pair_cols), jnp.float32),
-        ),
-    )
-    query = query.astype(jnp.bfloat16).astype(jnp.float32)
-    pair = pair.astype(jnp.bfloat16).astype(jnp.float32)
+    query = query_acc[...].astype(jnp.bfloat16).astype(jnp.float32)
     for j in range(group):
         query_heads[:, j, :] = query[:, j * head_size : (j + 1) * head_size]
+    for s in range(batch):
+        scores_ref[s] = lax.dot_general(
+            query_heads[s].astype(jnp.bfloat16),
+            key_ref[s],
+            (((1,), (1,)), ((), ())),
+            preferred_element_type=jnp.float32,
+        )
+
+    block = 2048
+
+    def project(i, pair):
+        here = pl.ds(pl.multiple_of(i * block, block), block)
+        return pair + jnp.dot(
+            spread_ref[:, here], pair_all[here, :], preferred_element_type=jnp.float32
+        )
+
+    pair = lax.fori_loop(
+        0,
+        pair_all.shape[0] // block,
+        project,
+        jnp.zeros((2 * batch, pair_cols), jnp.float32),
+    )
+    pair = pair.astype(jnp.bfloat16).astype(jnp.float32)
 
     scale = head_size ** (-0.5)
     slots = key_ref.shape[1]
     position = lax.broadcasted_iota(jnp.int32, (group, slots), 1)
+    own_weights = []
     for s in range(batch):
-        heads = query_heads[s]
-        scores = (
-            lax.dot_general(
-                heads.astype(jnp.bfloat16),
-                key_ref[s],
-                (((1,), (1,)), ((), ())),
-                preferred_element_type=jnp.float32,
-            )
-            * scale
-        )
-        scores = jnp.where(position < length_ref[s, :, 0:1], scores, -jnp.inf)
-        own = jnp.sum(heads * pair[s : s + 1], axis=1, keepdims=True) * scale
+        scores = jnp.where(position < length_ref[s, :, 0:1], scores_ref[s] * scale, -jnp.inf)
+        own = jnp.sum(query_heads[s] * pair[s : s + 1], axis=1, keepdims=True) * scale
         top = jnp.maximum(jnp.max(scores, axis=1, keepdims=True), own)
         weights = jnp.exp(scores - top)
         own_weight = jnp.exp(own - top)
-        total = jnp.sum(weights, axis=1, keepdims=True) + own_weight
-        weights = (weights / total).astype(jnp.bfloat16)
-        own_weight = (own_weight / total).astype(jnp.bfloat16).astype(jnp.float32)
-        context = jnp.dot(weights, value_ref[s], preferred_element_type=jnp.float32)
-        context_heads[s] = context + own_weight * pair[batch + s : batch + s + 1]
+        share = 1.0 / (jnp.sum(weights, axis=1, keepdims=True) + own_weight)
+        weights_ref[s] = (weights * share).astype(jnp.bfloat16)
+        own_weights.append((own_weight * share).astype(jnp.bfloat16).astype(jnp.float32))
+    for s in range(batch):
+        context_heads[s] = (
+            jnp.dot(weights_ref[s], value_ref[s], preferred_element_type=jnp.float32)
+            + own_weights[s] * pair[batch + s : batch + s + 1]
+        )
     for j in range(group):
-        context_ref[:, j * head_size : (j + 1) * head_size] = context_heads[:, j, :].astype(
-            context_ref.dtype
+        context_hold[:, j * head_size : (j + 1) * head_size] = context_heads[:, j, :].astype(
+            context_hold.dtype
         )
+    context = pltpu.make_async_copy(context_hold, context_ref, context_sem)
+    context.start()
     for copy in stores:
         copy.wait()
-
-
-def finish(normed, spread, query_all, pair_all, keys, values, lengths):
-    batch, width = normed.shape
-    query_cols, pair_cols = query_all.shape[1], pair_all.shape[2]
-    head_size = keys.shape[2]
+    context.wait()
+
+
+def finish(query_acc, spread, query_all, pair_all, keys, values, lengths):
+    batch, query_cols = query_acc.shape
+    width, _, pair_cols = pair_all.shape
+    kind = query_all.dtype
+    slots, head_size = keys.shape[1], keys.shape[2]
     group = query_cols // head_size
     pair_flat = pair_all.reshape(2 * width, pair_cols)
-    anywhere = pl.BlockSpec(memory_space=pl.ANY)
     vmem = pl.BlockSpec(memory_space=pltpu.VMEM)
     shape = jax.ShapeDtypeStruct
     query_out, pair_out, context = pl.pallas_call(
         finish_kernel,
         out_shape=(
-            shape(query_all.shape, query_all.dtype),
-            shape(pair_flat.shape, pair_all.dtype),
-            shape((batch, query_cols), normed.dtype),
+            shape(query_all.shape, kind),
+            shape(pair_flat.shape, kind),
+            shape((batch, query_cols), kind),
         ),
         in_specs=[vmem] * 7,
-        out_specs=(
-            pl.BlockSpec(memory_space=pltpu.HBM),
-            pl.BlockSpec(memory_space=pltpu.HBM),
-            vmem,
-        ),
+        out_specs=(pl.BlockSpec(memory_space=pltpu.HBM),) * 3,
         scratch_shapes=[
             pltpu.VMEM((batch, group, head_size), jnp.float32),
+            pltpu.VMEM((batch, group, slots), jnp.float32),
+            pltpu.VMEM((batch, group, slots), kind),
             pltpu.VMEM((batch, group, head_size), jnp.float32),
+            pltpu.VMEM((batch, query_cols), kind),
             pltpu.SemaphoreType.DMA((2, 4)),
+            pltpu.SemaphoreType.DMA(()),
         ],
         compiler_params=pltpu.CompilerParams(vmem_limit_bytes=8 * 2**20),
         cost_estimate=pl.CostEstimate(
-            flops=2 * batch * width * (query_cols + 4 * pair_cols),
+            flops=8 * batch * width * pair_cols,
             bytes_accessed=4 * width * (query_cols + 2 * pair_cols),
             transcendentals=0,
         ),
-        name="project_attend_store",
-    )(normed, spread, query_all, pair_flat, keys, values, lengths)
+        name="attend_and_store",
+    )(query_acc, spread, query_all, pair_flat, keys, values, lengths)
     return context, query_out, pair_out.reshape(width, 2, pair_cols)
 
 
@@ -762,7 +761,7 @@
     value_cache,
     cache_lengths,
 ):
-    query_all, pair_all, keys, values, lengths, normed, spread = exchange(
+    query_all, pair_all, keys, values, lengths, _, spread, query_acc = exchange(
         token_ids,
         norm_gain,
         embed_table,
@@ -773,7 +772,7 @@
         cache_lengths,
         planes,
     )
-    return finish(normed, spread, query_all, pair_all, keys, values, lengths)
+    return finish(query_acc, spread, query_all, pair_all, keys, values, lengths)
 
 
 def solution(mesh):

time: 197 us -> 188 us (0.954)
  Pallas kernels: 196 us -> 187 us
    pallas_call x1, Pallas kernels: 11.7 us -> 7.17 us  [finish(): pl.pallas_call(finish_kernel, out_shape=(shape(query_all.shape, kind), sh...]
    pallas_call x1, Pallas kernels: 185 us -> 180 us  [exchange(): pl.pallas_call(functools.partial(exchange_kernel, planes, subs), out_shap...]
where the time goes in v2:
time: 188 us
  Pallas kernels  187 us (99%)
    pallas_call x1, Pallas kernels, exchange(): pl.pallas_call(functools.partial(exchange_kernel, planes, subs), out_shap...  180 us
    pallas_call x1, Pallas kernels, finish(): pl.pallas_call(finish_kernel, out_shape=(shape(query_all.shape, kind), sh...  7.17 us

profile of v2, /device:TPU:1, one launch (start us, length us, event | category | flops | bytes accessed | tf_op | source)
XLA Modules:
  0.0 188.0 jit_solution(16391886904677338782)
XLA Ops:
  0.6 180.2 %weight_exchange.1 = (bf16[8192,1024]{1,0:T(8,128)(2,1)S(1)}, bf16[8192,2,128]{2,1,0:T(2,128)(2,1)S(1)}, bf16[16,1024,128]{2,1,0:T(8,128)(2,1)S(1)}, bf16[16,102...) custom-call(s32[1,128]{1,0:T(1,128)} %bitcast.7, ...), custom_call_target="tpu_custom_call" | custom-call | flops 199999995904 | bytes 16777216 | tf_op jit(solution)/shard_map/weight_exchange/pallas_call | solution.py:565
  180.9 7.2 %attend_and_store.1 = (bf16[8192,1024]{1,0:T(8,128)(2,1)}, bf16[16384,128]{1,0:T(8,128)(2,1)}, bf16[16,1024]{1,0:T(8,128)(2,1)}) custom-call(f32[16,1024]{1,0:T(8,128)S(1)} %get-tuple-element.13.query_acc, bf16[32,16384]{1,0:T(8,128)(2,1)S(1)} %get-tuple-element.14.spread_ref, bf16[8192,1024]{1,0:T(8,128)(2,1)S(1)} %get-tuple-element.15.query_all, ...), custom_call_target="tpu_custom_call" | custom-call | flops 134217728 | bytes 41943040 | tf_op jit(solution)/shard_map/attend_and_store/pallas_call | solution.py:724

commit v3 on v2

--- a/solution.py
+++ b/solution.py
@@ -110,7 +110,7 @@
 
 def exchange_kernel(
     planes,
-    subs,
+    cuts,
     token_in,
     gain_in,
     length_in,
@@ -150,6 +150,7 @@
     sum_recv,
     piece_send,
     piece_recv,
+    corner_sem,
 ):
     r, t = lax.axis_index("replica"), lax.axis_index("tp")
     replicas = 2 * planes
@@ -157,7 +158,7 @@
     ty, tx = t // 2, lax.rem(t, 2)
     rows, query_cols = query_in.shape[0], query_out.shape[1]
     pair_cols = pair_out.shape[2]
-    sub = rows // subs
+    finest = max(cuts.values())
     batch, feats = pieces.shape[1], pieces.shape[2]
     other = [t, ty * 2 + 1 - tx, (1 - ty) * 2 + tx, 3 - t]
     partner = z * 2 + 1 - k
@@ -165,7 +166,8 @@
     def piece_id(plane, core, tp):
         return (plane * 2 + core) * 4 + tp
 
-    def part_of(ref, pid, s):
+    def part_of(ref, pid, s, cut):
+        sub = rows // cut
         return ref.at[pl.ds(pl.multiple_of(pid * rows + s * sub, sub), sub)]
 
     mine = piece_id(z, k, t)
@@ -198,7 +200,7 @@
         copy.start()
 
     barrier = pltpu.get_barrier_semaphore()
-    for j in range(1, 4):
+    for j in range(1, 3):
         pl.semaphore_signal(barrier, inc=1, device_id=(r, other[j]), device_id_type=MESH)
     pl.semaphore_signal(barrier, inc=1, device_id=(partner, t), device_id_type=MESH)
     above, below = lax.rem(r + 2, replicas), lax.rem(r + replicas - 2, replicas)
@@ -213,83 +215,86 @@
 
     for copy in fetch[:2]:
         copy.start()
-    pl.semaphore_wait(barrier, 4 + jnp.minimum(z, 1) + jnp.minimum(planes - 1 - z, 1))
-
-    def landed(pid, s):
-        for c, out in enumerate((query_out, pair_out)):
-            place = part_of(out, pid, s)
-            pltpu.make_async_copy(place, place, recv_sem.at[c, pid * subs + s]).wait()
-
-    def send(pid, s, way, target):
-        for c, out in enumerate((query_out, pair_out)):
-            pltpu.make_async_remote_copy(
-                src_ref=part_of(out, pid, s),
-                dst_ref=part_of(out, pid, s),
-                send_sem=send_sem.at[c, way],
-                recv_sem=hand_recv.at[c, pid] if way == 2 else recv_sem.at[c, pid * subs + s],
-                device_id=target,
-                device_id_type=MESH,
-            ).start()
+    pl.semaphore_wait(barrier, 3 + jnp.minimum(z, 1) + jnp.minimum(planes - 1 - z, 1))
+
+    held = (query_out, pair_out)
+
+    def landed(c, pid, s, cut):
+        place = part_of(held[c], pid, s, cut)
+        pltpu.make_async_copy(place, place, recv_sem.at[c, pid * finest + s]).wait()
+
+    def send(c, pid, s, cut, way, target):
+        place = part_of(held[c], pid, s, cut)
+        pltpu.make_async_remote_copy(
+            src_ref=place,
+            dst_ref=place,
+            send_sem=send_sem.at[c, way],
+            recv_sem=hand_recv.at[c, pid] if way == 2 else recv_sem.at[c, pid * finest + s],
+            device_id=target,
+            device_id_type=MESH,
+        ).start()
 
     def sent(way, pieces_sent):
-        for c, out in enumerate((query_out, pair_out)):
+        for c, out in enumerate(held):
             place = out.at[0 : pieces_sent * rows]
             pltpu.make_async_copy(place, place, send_sem.at[c, way]).wait()
 
     def handed(pid):
-        for c, out in enumerate((query_out, pair_out)):
+        for c, out in enumerate(held):
             place = out.at[pl.ds(pl.multiple_of(pid * rows, rows), rows)]
             pltpu.make_async_copy(place, place, hand_recv.at[c, pid]).wait()
 
-    def across(j, s):
-        return [
-            pltpu.make_async_remote_copy(
-                src_ref=source,
-                dst_ref=part_of(out, mine, s),
-                send_sem=across_sem.at[c],
-                recv_sem=recv_sem.at[c, mine * subs + s],
-                device_id=(r, other[j]),
-                device_id_type=MESH,
-            )
-            for c, (source, out) in enumerate(
-                zip(
-                    columns(other[j], pl.multiple_of(s * sub, sub), sub),
-                    (query_out, pair_out),
-                )
-            )
-        ]
-
-    def onward(pid, s, up, down):
-        if up:
-
-            @pl.when(z < planes - 1)
-            def _():
-                send(pid, s, 0, (above, t))
-
-        if down:
-
-            @pl.when(z > 0)
-            def _():
-                send(pid, s, 1, (below, t))
-
-        send(pid, s, 2, (partner, t))
-
-    def each_sub(act):
-        def body(s, carry):
-            act(s)
+    def across(j):
+        cut = cuts["across", j]
+        sub = rows // cut
+
+        def act(s, carry):
+            sources = columns(other[j], pl.multiple_of(s * sub, sub), sub)
+            for c, source in enumerate(sources):
+                pltpu.make_async_remote_copy(
+                    src_ref=source,
+                    dst_ref=part_of(held[c], mine, s, cut),
+                    send_sem=across_sem.at[c],
+                    recv_sem=recv_sem.at[c, mine * finest + s],
+                    device_id=(r, other[j]),
+                    device_id_type=MESH,
+                ).start()
             return carry
 
-        lax.fori_loop(0, subs, body, 0)
+        lax.fori_loop(0, cut, act, 0)
+
+    def forward(pid, came_in, go_out, up, down):
+        groups = min(came_in, go_out) if came_in else go_out
+
+        def act(g, carry):
+            for c in range(2):
+                for i in range(came_in // groups):
+                    landed(c, pid, g * (came_in // groups) + i, came_in)
+                for i in range(go_out // groups):
+                    s = g * (go_out // groups) + i
+                    if up:
+
+                        @pl.when(z < planes - 1)
+                        def _():
+                            send(c, pid, s, go_out, 0, (above, t))
+
+                    if down:
+
+                        @pl.when(z > 0)
+                        def _():
+                            send(c, pid, s, go_out, 1, (below, t))
+
+                send(c, pid, g, groups, 2, (partner, t))
+            return carry
+
+        lax.fori_loop(0, groups, act, 0)
+
+    def out_cut(far, j):
+        return cuts.get((far, j), 1)
 
     def near(j):
-        pid = piece_id(z, k, other[j])
-
-        def act(s):
-            if j > 0:
-                landed(pid, s)
-            onward(pid, s, True, True)
-
-        each_sub(act)
+        came_in = cuts["across", j] if j else 0
+        forward(piece_id(z, k, other[j]), came_in, out_cut(0, j), True, True)
 
     def planes_at(far, act):
         if far == 0:
@@ -305,23 +310,21 @@
             act(lax.rem(z + far, planes), False)
 
     def far_away(far, j):
-        def forward(plane, up):
+        def act(plane, up):
             pid = piece_id(plane, k, other[j])
-
-            def act(s):
-                landed(pid, s)
-                onward(pid, s, up, not up)
-
-            each_sub(act)
-
-        planes_at(far, forward)
+            forward(pid, out_cut(far - 1, j), out_cut(far, j), up, not up)
+
+        planes_at(far, act)
 
     def multiply(far, j):
         def both(plane, up):
-            handed(piece_id(plane, 1 - k, other[j]))
-
-            def add(core, carry):
-                pid = piece_id(plane, core, other[j])
+            def add(turn, carry):
+                pid = piece_id(plane, jnp.where(turn == 0, k, 1 - k), other[j])
+
+                @pl.when(turn == 1)
+                def _():
+                    handed(pid)
+
                 where = pl.ds(pl.multiple_of(pid * rows, rows), rows)
                 query_acc[...] += jnp.dot(
                     normed_ref[:, where], query_out[where, :], preferred_element_type=jnp.float32
@@ -335,18 +338,14 @@
     for copy in bring:
         copy.wait()
 
-    def send_across(j):
-        def act(s):
-            for copy in across(j, s):
-                copy.start()
-
-        each_sub(act)
-
     near(0)
-    for j in range(1, 4):
-        send_across(j)
+    pl.semaphore_signal(corner_sem, inc=1, device_id=(r, other[1]), device_id_type=MESH)
+    across(1)
+    across(2)
     for copy in fetch[2:]:
         copy.start()
+    pl.semaphore_wait(corner_sem, 1)
+    across(3)
 
     gives = [
         pltpu.make_async_remote_copy(
@@ -557,13 +556,14 @@
     group = query_cols // head_size
     tokens = token_ids.shape[0]
     lanes = 128
-    subs = 2
+    cuts = {("across", 1): 1, ("across", 2): 1, ("across", 3): 1}
+    cuts |= {(0, 0): 1, (0, 1): 1, (0, 2): 1, (0, 3): 1}
     anywhere = pl.BlockSpec(memory_space=pl.ANY)
     vmem = pl.BlockSpec(memory_space=pltpu.VMEM)
     dma = pltpu.SemaphoreType.DMA
     shape = jax.ShapeDtypeStruct
     return pl.pallas_call(
-        functools.partial(exchange_kernel, planes, subs),
+        functools.partial(exchange_kernel, planes, cuts),
         out_shape=(
             pltpu.VMEM((width, query_cols), kind),
             pltpu.VMEM((width, 2, pair_cols), kind),
@@ -590,7 +590,7 @@
             pltpu.VMEM((2, planes, batch, feats), kind),
             pltpu.VMEM((4, batch, feats), kind),
             dma((2, 3)),
-            dma((2, replicas * 4 * subs)),
+            dma((2, replicas * 4 * max(cuts.values()))),
             dma((2, replicas * 4)),
             dma((2,)),
             dma((8,)),
@@ -600,6 +600,7 @@
             dma((2, planes)),
             dma((3,)),
             dma((3,)),
+            pltpu.SemaphoreType.REGULAR,
         ],
         compiler_params=pltpu.CompilerParams(
             collective_id=0, has_side_effects=True, vmem_limit_bytes=8 * 2**20

time: 188 us -> 186 us (0.989)
  no operation moved by 1% of the time
where the time goes in v3:
time: 186 us
  Pallas kernels  186 us (100%)
    pallas_call x1, Pallas kernels, exchange(): pl.pallas_call(functools.partial(exchange_kernel, planes, cuts), out_shap...  178 us
    pallas_call x1, Pallas kernels, finish(): pl.pallas_call(finish_kernel, out_shape=(shape(query_all.shape, kind), sh...  7.17 us

profile of v3, /device:TPU:1, one launch (start us, length us, event | category | flops | bytes accessed | tf_op | source)
XLA Modules:
  0.0 186.2 jit_solution(14131032159473011586)
XLA Ops:
  0.6 178.4 %weight_exchange.1 = (bf16[8192,1024]{1,0:T(8,128)(2,1)S(1)}, bf16[8192,2,128]{2,1,0:T(2,128)(2,1)S(1)}, bf16[16,1024,128]{2,1,0:T(8,128)(2,1)S(1)}, bf16[16,102...) custom-call(s32[1,128]{1,0:T(1,128)} %bitcast.7, ...), custom_call_target="tpu_custom_call" | custom-call | flops 199999995904 | bytes 16777216 | tf_op jit(solution)/shard_map/weight_exchange/pallas_call | solution.py:565
  179.0 7.2 %attend_and_store.1 = (bf16[8192,1024]{1,0:T(8,128)(2,1)}, bf16[16384,128]{1,0:T(8,128)(2,1)}, bf16[16,1024]{1,0:T(8,128)(2,1)}) custom-call(f32[16,1024]{1,0:T(8,128)S(1)} %get-tuple-element.13.query_acc, bf16[32,16384]{1,0:T(8,128)(2,1)S(1)} %get-tuple-element.14.spread_ref, bf16[8192,1024]{1,0:T(8,128)(2,1)S(1)} %get-tuple-element.15.query_all, ...), custom_call_target="tpu_custom_call" | custom-call | flops 134217728 | bytes 41943040 | tf_op jit(solution)/shard_map/attend_and_store/pallas_call | solution.py:725

commit v4 on v3

--- a/solution.py
+++ b/solution.py
@@ -170,6 +170,9 @@
         sub = rows // cut
         return ref.at[pl.ds(pl.multiple_of(pid * rows + s * sub, sub), sub)]
 
+    def slot(pid):
+        return (pid // 8) * 4 + lax.rem(pid, 4)
+
     mine = piece_id(z, k, t)
 
     def columns(tp, first, count):
@@ -221,7 +224,7 @@
 
     def landed(c, pid, s, cut):
         place = part_of(held[c], pid, s, cut)
-        pltpu.make_async_copy(place, place, recv_sem.at[c, pid * finest + s]).wait()
+        pltpu.make_async_copy(place, place, recv_sem.at[c, slot(pid) * finest + s]).wait()
 
     def send(c, pid, s, cut, way, target):
         place = part_of(held[c], pid, s, cut)
@@ -229,7 +232,9 @@
             src_ref=place,
             dst_ref=place,
             send_sem=send_sem.at[c, way],
-            recv_sem=hand_recv.at[c, pid] if way == 2 else recv_sem.at[c, pid * finest + s],
+            recv_sem=(
+                hand_recv.at[slot(pid)] if way == 2 else recv_sem.at[c, slot(pid) * finest + s]
+            ),
             device_id=target,
             device_id_type=MESH,
         ).start()
@@ -240,9 +245,8 @@
             pltpu.make_async_copy(place, place, send_sem.at[c, way]).wait()
 
     def handed(pid):
-        for c, out in enumerate(held):
-            place = out.at[pl.ds(pl.multiple_of(pid * rows, rows), rows)]
-            pltpu.make_async_copy(place, place, hand_recv.at[c, pid]).wait()
+        place = query_out.at[0 : rows + 2 * rows * pair_cols // query_cols]
+        pltpu.make_async_copy(place, place, hand_recv.at[slot(pid)]).wait()
 
     def across(j):
         cut = cuts["across", j]
@@ -255,7 +259,7 @@
                     src_ref=source,
                     dst_ref=part_of(held[c], mine, s, cut),
                     send_sem=across_sem.at[c],
-                    recv_sem=recv_sem.at[c, mine * finest + s],
+                    recv_sem=recv_sem.at[c, slot(mine) * finest + s],
                     device_id=(r, other[j]),
                     device_id_type=MESH,
                 ).start()
@@ -347,17 +351,14 @@
     pl.semaphore_wait(corner_sem, 1)
     across(3)
 
-    gives = [
-        pltpu.make_async_remote_copy(
-            src_ref=part_ref.at[plane, 1 - k],
-            dst_ref=given.at[plane],
-            send_sem=give_send.at[plane],
-            recv_sem=give_recv.at[plane],
-            device_id=(partner, t),
-            device_id_type=MESH,
-        )
-        for plane in range(planes)
-    ]
+    give = pltpu.make_async_remote_copy(
+        src_ref=part_ref.at[:, 1 - k],
+        dst_ref=given,
+        send_sem=give_send,
+        recv_sem=give_recv,
+        device_id=(partner, t),
+        device_id_type=MESH,
+    )
 
     last = planes - 1
 
@@ -430,8 +431,7 @@
         lax.fori_loop(0, feats // block, select, 0)
 
     def join():
-        for copy in gives:
-            copy.wait()
+        give.wait()
         for plane in range(planes):
             kept = part_ref[plane, k].astype(jnp.float32)
             joined[plane] = (kept + given[plane].astype(jnp.float32)).astype(jnp.bfloat16)
@@ -498,8 +498,7 @@
             length_out[s] = jnp.full((group, length_out.shape[2]), length_hold[s], jnp.int32)
 
     select_rows()
-    for copy in gives:
-        copy.start()
+    give.start()
     join()
     passing(0)
     order = [(0, 1), (0, 2), (1, 0), (0, 3)]
@@ -590,12 +589,12 @@
             pltpu.VMEM((2, planes, batch, feats), kind),
             pltpu.VMEM((4, batch, feats), kind),
             dma((2, 3)),
-            dma((2, replicas * 4 * max(cuts.values()))),
-            dma((2, replicas * 4)),
+            dma((2, replicas * 2 * max(cuts.values()))),
+            dma((replicas * 2,)),
             dma((2,)),
             dma((8,)),
-            dma((planes,)),
-            dma((planes,)),
+            dma(()),
+            dma(()),
             dma((2, planes)),
             dma((2, planes)),
             dma((3,)),

time: 186 us -> 186 us (level)
  no operation moved by 1% of the time
where the time goes in v4:
time: 186 us; the launch traced here: 185 us
  Pallas kernels  185 us (99%)
    pallas_call x1, Pallas kernels, exchange(): pl.pallas_call(functools.partial(exchange_kernel, planes, cuts), out_shap...  178 us
    pallas_call x1, Pallas kernels, finish(): pl.pallas_call(finish_kernel, out_shape=(shape(query_all.shape, kind), sh...  7.17 us

profile of v4, /device:TPU:1, one launch (start us, length us, event | category | flops | bytes accessed | tf_op | source)
XLA Modules:
  0.0 185.4 jit_solution(4452052741718408907)
XLA Ops:
  0.6 177.6 %weight_exchange.1 = (bf16[8192,1024]{1,0:T(8,128)(2,1)S(1)}, bf16[8192,2,128]{2,1,0:T(2,128)(2,1)S(1)}, bf16[16,1024,128]{2,1,0:T(8,128)(2,1)S(1)}, bf16[16,102...) custom-call(s32[1,128]{1,0:T(1,128)} %bitcast.7, ...), custom_call_target="tpu_custom_call" | custom-call | flops 199999995904 | bytes 16777216 | tf_op jit(solution)/shard_map/weight_exchange/pallas_call | solution.py:564
  178.2 7.2 %attend_and_store.1 = (bf16[8192,1024]{1,0:T(8,128)(2,1)}, bf16[16384,128]{1,0:T(8,128)(2,1)}, bf16[16,1024]{1,0:T(8,128)(2,1)}) custom-call(f32[16,1024]{1,0:T(8,128)S(1)} %get-tuple-element.13.query_acc, bf16[32,16384]{1,0:T(8,128)(2,1)S(1)} %get-tuple-element.14.spread_ref, bf16[8192,1024]{1,0:T(8,128)(2,1)S(1)} %get-tuple-element.15.query_all, ...), custom_call_target="tpu_custom_call" | custom-call | flops 134217728 | bytes 41943040 | tf_op jit(solution)/shard_map/attend_and_store/pallas_call | solution.py:724

commit v5 on v4

--- a/solution.py
+++ b/solution.py
@@ -124,9 +124,9 @@
     key_out,
     value_out,
     length_out,
-    normed_ref,
     spread_ref,
     query_acc,
+    normed_ref,
     token_hold,
     gain_hold,
     gain_wide,
@@ -569,13 +569,13 @@
             pltpu.VMEM(key_cache.shape, kind),
             pltpu.VMEM(value_cache.shape, kind),
             pltpu.VMEM((batch, group, head_size), jnp.int32),
-            pltpu.VMEM((batch, width), kind),
             pltpu.VMEM((2 * batch, 2 * width), kind),
             pltpu.VMEM((batch, query_cols), jnp.float32),
         ),
         in_specs=[anywhere] * 8,
-        out_specs=(vmem,) * 8,
+        out_specs=(vmem,) * 7,
         scratch_shapes=[
+            pltpu.VMEM((batch, width), kind),
             pltpu.VMEM((1, tokens), jnp.int32),
             pltpu.VMEM((width // lanes, lanes), kind),
             pltpu.VMEM((width // lanes, lanes), jnp.float32),
@@ -761,7 +761,7 @@
     value_cache,
     cache_lengths,
 ):
-    query_all, pair_all, keys, values, lengths, _, spread, query_acc = exchange(
+    query_all, pair_all, keys, values, lengths, spread, query_acc = exchange(
         token_ids,
         norm_gain,
         embed_table,

time: 186 us -> 185 us (level)
  no operation moved by 1% of the time
where the time goes in v5:
time: 185 us
  Pallas kernels  184 us (99%)
    pallas_call x1, Pallas kernels, exchange(): pl.pallas_call(functools.partial(exchange_kernel, planes, cuts), out_shap...  177 us
    pallas_call x1, Pallas kernels, finish(): pl.pallas_call(finish_kernel, out_shape=(shape(query_all.shape, kind), sh...  7.17 us

profile of v5, /device:TPU:1, one launch (start us, length us, event | category | flops | bytes accessed | tf_op | source)
XLA Modules:
  0.0 184.7 jit_solution(7066785390248225928)
XLA Ops:
  0.6 176.9 %weight_exchange.1 = (bf16[8192,1024]{1,0:T(8,128)(2,1)S(1)}, bf16[8192,2,128]{2,1,0:T(2,128)(2,1)S(1)}, bf16[16,1024,128]{2,1,0:T(8,128)(2,1)S(1)}, bf16[16,102...) custom-call(s32[1,128]{1,0:T(1,128)} %bitcast.7, ...), custom_call_target="tpu_custom_call" | custom-call | flops 199999995904 | bytes 16777216 | tf_op jit(solution)/shard_map/weight_exchange/pallas_call | solution.py:564
  177.5 7.2 %attend_and_store.1 = (bf16[8192,1024]{1,0:T(8,128)(2,1)}, bf16[16384,128]{1,0:T(8,128)(2,1)}, bf16[16,1024]{1,0:T(8,128)(2,1)}) custom-call(f32[16,1024]{1,0:T(8,128)S(1)} %get-tuple-element.13.query_acc, bf16[32,16384]{1,0:T(8,128)(2,1)S(1)} %get-tuple-element.14.spread_ref, bf16[8192,1024]{1,0:T(8,128)(2,1)S(1)} %get-tuple-element.15.query_all, ...), custom_call_target="tpu_custom_call" | custom-call | flops 134217728 | bytes 41943040 | tf_op jit(solution)/shard_map/attend_and_store/pallas_call | solution.py:724
